TPU v7x, 32 devices: a whole 2x2x4 slice. The times are simulated.
32 devices in a mesh: dp: 4 (over x, core), head: 8 (over z, y).
Axes of the slice: x: 2, y: 2, z: 4, core: 2. Of those that a mesh axis runs over, the one named last changes fastest.
Arguments:
- tokens: bfloat16 [24576, 1152], P(('dp', 'head')), may hold values from -6 to 6
- segment_ids: int32 [24576], P('dp'), may hold values from 0 to 95, as said below
- cond: float32 [96, 1152], P('dp'), may hold values from -6 to 6
- w_ada: bfloat16 [1152, 6912], P(None, 'head'), may hold values from -0.1875 to 0.1875
- b_ada: bfloat16 [6912], P('head'), may hold values from -4 to 4
- w_qkv: bfloat16 [1152, 3, 1152], P(None, None, 'head'), may hold values from -0.1875 to 0.1875
- bias_qv: bfloat16 [2, 1152], P(None, 'head'), may hold values from -4 to 4
- w_proj: bfloat16 [1152, 1152], P('head'), may hold values from -0.75 to 0.75
- b_proj: bfloat16 [1152], replicated, may hold values from -4 to 4
- w_fc1: bfloat16 [1152, 4608], P(None, 'head'), may hold values from -0.1875 to 0.1875
- b_fc1: bfloat16 [4608], P('head'), may hold values from -4 to 4
- w_fc2: bfloat16 [4608, 1152], P('head'), may hold values from -0.09375 to 0.09375
- b_fc2: bfloat16 [1152], replicated, may hold values from -4 to 4
- cotangent: bfloat16 [24576, 1152], P(('dp', 'head')), may hold values from -6 to 6
Outputs:
- out: bfloat16 [24576, 1152], P(('dp', 'head'))
- grad_tokens: bfloat16 [24576, 1152], P(('dp', 'head'))
- grad_cond: float32 [96, 1152], P('dp')
- grad_w_ada: float32 [1152, 6912], P(None, 'head')
- grad_b_ada: float32 [6912], P('head')
- grad_w_qkv: float32 [1152, 3, 1152], P(None, None, 'head')
- grad_bias_qv: float32 [2, 1152], P(None, 'head')
- grad_w_proj: float32 [1152, 1152], P('head')
- grad_b_proj: float32 [1152], replicated
- grad_w_fc1: float32 [1152, 4608], P(None, 'head')
- grad_b_fc1: float32 [4608], P('head')
- grad_w_fc2: float32 [4608, 1152], P('head')
- grad_b_fc2: float32 [1152], replicated
Inputs may be any that keep to these rules, and one draw needn't show every extreme that they name: `segment_ids`: each packed row of 2048 consecutive tokens is two halves of 1024 tokens, each either one segment or segments of 256 tokens. The ids of the tokens of index g of dp lie in g * 24 onward; a segment's id is that base plus (its first position within those tokens) // 256, so ids never fall and some slots name no token. In the last packed row of every index of dp the first half is one segment and the second half is split.
All inputs are finite; a program needn't handle non-finite values.
Results may differ from a plain program's by a relative error of at most 0.019.
The roundings to bfloat16 on the way count: a program that leaves them out, or rounds other values in their place, can miss the bound.
Values may be sent and summed in bfloat16 or wider, within the bound.
A program may use at most 320 MiB of HBM per device.

v0:
```python
import math

import jax
import jax.numpy as jnp
from jax import lax
from jax.sharding import PartitionSpec as P

HEAD_DIM = 72
PACK = 2048


norm_eps = 1e-06
top_precision = lax.Precision.HIGHEST


def layer_norm(values):
    centered = values - jnp.mean(values, axis=-1, keepdims=True)
    inverse = lax.rsqrt(jnp.mean(centered * centered, axis=-1, keepdims=True) + norm_eps)
    return (centered * inverse, inverse)


def norm_back(grad_normed, normed, inverse):
    mean_grad = jnp.mean(grad_normed, axis=-1, keepdims=True)
    mean_cross = jnp.mean(grad_normed * normed, axis=-1, keepdims=True)
    return inverse * (grad_normed - mean_grad - normed * mean_cross)


def gelu_tanh(values):
    return jax.nn.gelu(values, approximate=True)


def block_setup(query_row, key_row, value_row, head_width):
    length, columns = query_row.shape
    heads_here = columns // head_width
    block_rows = min(512, length)
    blocks = length // block_rows
    keys_split = key_row.reshape(length, heads_here, head_width)
    values_split = value_row.reshape(length, heads_here, head_width)
    queries_split = query_row.reshape(blocks, block_rows, heads_here, head_width)
    return (block_rows, blocks, keys_split, values_split, queries_split)


def row_forward(query_row, key_row, value_row, ident_row, head_width):
    block_rows, blocks, keys_split, values_split, queries_split = block_setup(
        query_row, key_row, value_row, head_width
    )
    scale = 1.0 / math.sqrt(head_width)
    ident_blocks = ident_row.reshape(blocks, block_rows)

    def one_block(inputs):
        query_block, ident_block = inputs
        scores = (
            jnp.einsum("qhd,khd->hqk", query_block, keys_split, preferred_element_type=jnp.float32)
            * scale
        )
        allowed = (ident_block[:, None] == ident_row[None, :])[None]
        scores = jnp.where(allowed, scores, -1e30)
        highest = jnp.max(scores, axis=-1, keepdims=True)
        weights = jnp.exp(scores - highest)
        totals = jnp.sum(weights, axis=-1, keepdims=True)
        probs = (weights / totals).astype(jnp.bfloat16)
        mixed = jnp.einsum("hqk,khd->qhd", probs, values_split, preferred_element_type=jnp.float32)
        return (
            mixed.reshape(block_rows, -1).astype(jnp.bfloat16),
            (highest + jnp.log(totals))[..., 0],
        )

    mixed, log_totals = lax.map(one_block, (queries_split, ident_blocks))
    return (mixed.reshape(query_row.shape), log_totals)


def row_backward(query_row, key_row, value_row, ident_row, log_row, grad_row, head_width):
    block_rows, blocks, keys_split, values_split, queries_split = block_setup(
        query_row, key_row, value_row, head_width
    )
    heads_here = keys_split.shape[1]
    scale = 1.0 / math.sqrt(head_width)
    grads_split = grad_row.reshape(blocks, block_rows, heads_here, head_width)
    ident_blocks = ident_row.reshape(blocks, block_rows)

    def one_block(carry, inputs):
        key_total, value_total = carry
        query_block, grad_block, ident_block, log_block = inputs
        scores = (
            jnp.einsum("qhd,khd->hqk", query_block, keys_split, preferred_element_type=jnp.float32)
            * scale
        )
        allowed = (ident_block[:, None] == ident_row[None, :])[None]
        probs = jnp.where(allowed, jnp.exp(scores - log_block[:, :, None]), 0.0)
        grad_probs = jnp.einsum(
            "qhd,khd->hqk", grad_block, values_split, preferred_element_type=jnp.float32
        )
        inner = jnp.sum(probs * grad_probs, axis=-1, keepdims=True)
        grad_scores = (probs * (grad_probs - inner)).astype(jnp.bfloat16)
        grad_query = (
            jnp.einsum("hqk,khd->qhd", grad_scores, keys_split, preferred_element_type=jnp.float32)
            * scale
        )
        key_total = (
            key_total
            + jnp.einsum(
                "hqk,qhd->khd", grad_scores, query_block, preferred_element_type=jnp.float32
            )
            * scale
        )
        value_total = value_total + jnp.einsum(
            "hqk,qhd->khd",
            probs.astype(jnp.bfloat16),
            grad_block,
            preferred_element_type=jnp.float32,
        )
        return ((key_total, value_total), grad_query.reshape(block_rows, -1).astype(jnp.bfloat16))

    zero_total = jnp.zeros(keys_split.shape, jnp.float32)
    (key_total, value_total), grad_query = lax.scan(
        one_block, (zero_total, zero_total), (queries_split, grads_split, ident_blocks, log_row)
    )
    length = ident_row.shape[0]
    return (
        grad_query.reshape(length, -1),
        key_total.reshape(length, -1).astype(jnp.bfloat16),
        value_total.reshape(length, -1).astype(jnp.bfloat16),
    )


def attend(query, keys, values, idents):
    packed = idents.shape[0] // PACK

    def one_row(inputs):
        return row_forward(inputs[0], inputs[1], inputs[2], inputs[3], HEAD_DIM)

    mixed, log_totals = lax.map(
        one_row,
        (
            query.reshape(packed, PACK, -1),
            keys.reshape(packed, PACK, -1),
            values.reshape(packed, PACK, -1),
            idents.reshape(packed, PACK),
        ),
    )
    return (mixed.reshape(query.shape), log_totals)


def attend_back(query, keys, values, idents, log_totals, grad_mix):
    packed = idents.shape[0] // PACK

    def one_row(inputs):
        return row_backward(
            inputs[0], inputs[1], inputs[2], inputs[3], inputs[4], inputs[5], HEAD_DIM
        )

    grad_query, grad_key, grad_value = lax.map(
        one_row,
        (
            query.reshape(packed, PACK, -1),
            keys.reshape(packed, PACK, -1),
            values.reshape(packed, PACK, -1),
            idents.reshape(packed, PACK),
            log_totals,
            grad_mix.reshape(packed, PACK, -1),
        ),
    )
    return (
        grad_query.reshape(query.shape),
        grad_key.reshape(query.shape),
        grad_value.reshape(query.shape),
    )


def local(
    tokens,
    segment_ids,
    cond,
    w_ada,
    b_ada,
    w_qkv,
    bias_qv,
    w_proj,
    b_proj,
    w_fc1,
    b_fc1,
    w_fc2,
    b_fc2,
    cotangent,
):
    rows_here, width = tokens.shape
    slots = cond.shape[0]
    columns = w_qkv.shape[2]
    row_start = lax.axis_index("head") * rows_here
    own_ids = (
        lax.dynamic_slice_in_dim(segment_ids, row_start, rows_here) - lax.axis_index("dp") * slots
    )
    pick = (own_ids[:, None] == jnp.arange(slots, dtype=jnp.int32)[None, :]).astype(jnp.float32)
    cond_act, silu_back = jax.vjp(jax.nn.silu, cond)
    cond_low = cond_act.astype(jnp.bfloat16)
    mod_part = jnp.dot(cond_low, w_ada, preferred_element_type=jnp.float32) + b_ada.astype(
        jnp.float32
    )
    modulation = lax.all_gather(mod_part, "head", axis=1, tiled=True)
    per_token = jnp.dot(pick, modulation, precision=top_precision)
    shift_a, scale_a, gate_a, shift_m, scale_m, gate_m = jnp.split(per_token, 6, axis=1)
    resid = tokens.astype(jnp.float32)
    normed_a, inverse_a = layer_norm(resid)
    attn_in = (normed_a * (1.0 + scale_a) + shift_a).astype(jnp.bfloat16)
    gathered_a = lax.all_gather(attn_in, "head", axis=0, tiled=True)
    qkv_weight = w_qkv.reshape(width, 3 * columns)
    qkv_bias = jnp.concatenate(
        [bias_qv[0], jnp.zeros((columns,), bias_qv.dtype), bias_qv[1]]
    ).astype(jnp.float32)
    qkv = (jnp.dot(gathered_a, qkv_weight, preferred_element_type=jnp.float32) + qkv_bias).astype(
        jnp.bfloat16
    )
    query = qkv[:, :columns]
    keys = qkv[:, columns : 2 * columns]
    values = qkv[:, 2 * columns :]
    attn_mix, log_totals = attend(query, keys, values, segment_ids)
    branch_a = lax.psum_scatter(
        jnp.dot(attn_mix, w_proj, preferred_element_type=jnp.float32),
        "head",
        scatter_dimension=0,
        tiled=True,
    ) + b_proj.astype(jnp.float32)
    mid = resid + gate_a * branch_a
    normed_m, inverse_m = layer_norm(mid)
    mlp_in = (normed_m * (1.0 + scale_m) + shift_m).astype(jnp.bfloat16)
    cotan = cotangent.astype(jnp.float32)
    grad_branch_m = (gate_m * cotan).astype(jnp.bfloat16)
    gathered_m = lax.all_gather(mlp_in, "head", axis=0, tiled=True)
    pre = jnp.dot(gathered_m, w_fc1, preferred_element_type=jnp.float32) + b_fc1.astype(jnp.float32)
    hidden, gelu_back = jax.vjp(gelu_tanh, pre)
    hidden_low = hidden.astype(jnp.bfloat16)
    branch_m = lax.psum_scatter(
        jnp.dot(hidden_low, w_fc2, preferred_element_type=jnp.float32).astype(jnp.bfloat16),
        "head",
        scatter_dimension=0,
        tiled=True,
    ).astype(jnp.float32) + b_fc2.astype(jnp.float32)
    grad_rows_m = lax.all_gather(grad_branch_m, "head", axis=0, tiled=True)
    grad_hidden = jnp.einsum("td,fd->tf", grad_rows_m, w_fc2, preferred_element_type=jnp.float32)
    grad_pre = gelu_back(grad_hidden)[0].astype(jnp.bfloat16)
    grad_fc1 = jnp.einsum("td,tf->df", gathered_m, grad_pre, preferred_element_type=jnp.float32)
    grad_fc2 = jnp.einsum("tf,td->fd", hidden_low, grad_rows_m, preferred_element_type=jnp.float32)
    grad_b1 = jnp.sum(grad_pre.astype(jnp.float32), axis=0)
    grad_mlp_in = lax.psum_scatter(
        jnp.einsum("tf,df->td", grad_pre, w_fc1, preferred_element_type=jnp.float32),
        "head",
        scatter_dimension=0,
        tiled=True,
    )
    output = (mid + gate_m * branch_m).astype(jnp.bfloat16)
    grad_mid = cotan + norm_back(grad_mlp_in * (1.0 + scale_m), normed_m, inverse_m)
    grad_branch_a = (gate_a * grad_mid).astype(jnp.bfloat16)
    grad_rows_a = lax.all_gather(grad_branch_a, "head", axis=0, tiled=True)
    grad_proj = jnp.einsum("tc,td->cd", attn_mix, grad_rows_a, preferred_element_type=jnp.float32)
    grad_mix = jnp.einsum(
        "td,cd->tc", grad_rows_a, w_proj, preferred_element_type=jnp.float32
    ).astype(jnp.bfloat16)
    grad_query, grad_key, grad_value = attend_back(
        query, keys, values, segment_ids, log_totals, grad_mix
    )
    grad_qkv = jnp.concatenate([grad_query, grad_key, grad_value], axis=1)
    grad_w_qkv = jnp.einsum(
        "td,tc->dc", gathered_a, grad_qkv, preferred_element_type=jnp.float32
    ).reshape(width, 3, columns)
    grad_bias_qv = jnp.stack(
        [
            jnp.sum(grad_query.astype(jnp.float32), axis=0),
            jnp.sum(grad_value.astype(jnp.float32), axis=0),
        ]
    )
    grad_attn_in = lax.psum_scatter(
        jnp.einsum("tc,dc->td", grad_qkv, qkv_weight, preferred_element_type=jnp.float32).astype(
            jnp.bfloat16
        ),
        "head",
        scatter_dimension=0,
        tiled=True,
    ).astype(jnp.float32)
    grad_tokens = (
        grad_mid + norm_back(grad_attn_in * (1.0 + scale_a), normed_a, inverse_a)
    ).astype(jnp.bfloat16)
    per_token_grad = jnp.concatenate(
        [
            grad_attn_in,
            grad_attn_in * normed_a,
            grad_mid * branch_a,
            grad_mlp_in,
            grad_mlp_in * normed_m,
            cotan * branch_m,
        ],
        axis=1,
    )
    grad_mod_part = jnp.einsum("ts,tm->sm", pick, per_token_grad, precision=top_precision)
    grad_mod = lax.psum_scatter(
        grad_mod_part.astype(jnp.bfloat16), "head", scatter_dimension=1, tiled=True
    ).astype(jnp.float32)
    grad_w_ada = jnp.einsum(
        "sd,sm->dm", cond_low.astype(jnp.float32), grad_mod, precision=top_precision
    )
    grad_b_ada = jnp.sum(grad_mod, axis=0)
    grad_cond_part = jnp.einsum(
        "sm,dm->sd", grad_mod, w_ada.astype(jnp.float32), precision=top_precision
    )
    proj_bias_part = jnp.sum(grad_branch_a.astype(jnp.float32), axis=0)
    mlp_bias_part = jnp.sum(grad_branch_m.astype(jnp.float32), axis=0)
    grad_cond_act, grad_b_proj, grad_b2 = (
        lax.psum(grad_cond_part.astype(jnp.bfloat16), "head").astype(jnp.float32),
        lax.psum(proj_bias_part.astype(jnp.bfloat16), "head").astype(jnp.float32),
        lax.psum(mlp_bias_part.astype(jnp.bfloat16), "head").astype(jnp.float32),
    )
    grad_cond = silu_back(grad_cond_act)[0]
    summed = (
        lax.psum(grad_w_ada.astype(jnp.bfloat16), "dp").astype(jnp.float32),
        lax.psum(grad_b_ada.astype(jnp.bfloat16), "dp").astype(jnp.float32),
        lax.psum(grad_w_qkv.astype(jnp.bfloat16), "dp").astype(jnp.float32),
        lax.psum(grad_bias_qv.astype(jnp.bfloat16), "dp").astype(jnp.float32),
        lax.psum(grad_proj.astype(jnp.bfloat16), "dp").astype(jnp.float32),
        lax.psum(grad_b_proj.astype(jnp.bfloat16), "dp").astype(jnp.float32),
        lax.psum(grad_fc1.astype(jnp.bfloat16), "dp").astype(jnp.float32),
        lax.psum(grad_b1.astype(jnp.bfloat16), "dp").astype(jnp.float32),
        lax.psum(grad_fc2.astype(jnp.bfloat16), "dp").astype(jnp.float32),
        lax.psum(grad_b2.astype(jnp.bfloat16), "dp").astype(jnp.float32),
    )
    return (output, grad_tokens, grad_cond) + tuple(summed)


def solution(mesh):
    placed = (
        P(("dp", "head"), None),
        P("dp"),
        P("dp", None),
        P(None, "head"),
        P("head"),
        P(None, None, "head"),
        P(None, "head"),
        P("head", None),
        P(),
        P(None, "head"),
        P("head"),
        P("head", None),
        P(),
        P(("dp", "head"), None),
    )
    return jax.shard_map(
        local,
        mesh=mesh,
        in_specs=placed,
        out_specs=(
            P(("dp", "head"), None),
            P(("dp", "head"), None),
            P("dp", None),
            P(None, "head"),
            P("head"),
            P(None, None, "head"),
            P(None, "head"),
            P("head", None),
            P(),
            P(None, "head"),
            P("head"),
            P("head", None),
            P(),
        ),
        check_vma=False,
    )
```

profile of v0, /device:TPU:0, one launch (start us, length us, event | category | flops | bytes accessed | tf_op | source)
XLA Modules:
  0.0 2927.1 jit_solution(12163566460413241053)
XLA Ops:
  12.7 33.5 %all-gather = f32[8,864,24]{1,2,0:T(8,128)S(1)} all-gather(f32[1,864,24]{1,2,0:T(8,128)S(1)} %fusion.64), channel_id=1, replica_groups=mesh['dp'=4,'head'=8] {'head'}, dimensions={0}, use_global_device_ids=true | all-gather | bytes 746496 | tf_op jit(solution)/shard_map/all_gather | solution.py:199
  65.1 195.9 %all-gather.6.cloned.1.call-done = bf16[6144,1152]{1,0:T(8,128)(2,1)} async-done(((bf16[768,1152]{1,0:T(8,128)(2,1)}), bf16[6144,1152]{1,0:T(8,128)(2,1)}) %all-gather.6.cloned.1.call-update) | async-done | bytes 14155792 | tf_op jit(solution)/shard_map/all_gather | solution.py:205
  277.1 140.8 %while.54 = (s32[]{:T(128)}, bf16[3,2048,144]{2,1,0:T(8,128)(2,1)}, f32[3,4,2,512]{3,2,1,0:T(2,128)}, bf16[3,2048,144]{1,2,0:T(8,128)(2,1)}, s32[3,2048]{1,0:T(4...) while((s32[]{:T(128)}, bf16[3,2048,144]{2,1,0:T(8,128)(2,1)}, ...), condition=%wide.region_7.8_spmd, body=%wide.region_2.7_spmd.sunk | while | flops 630266880 | bytes 39967056 | solution.py:132
  282.1 38.9 %while.57 = (s32[]{:T(128)}, bf16[4,512,144]{1,2,0:T(8,128)(2,1)}, f32[4,2,512]{2,1,0:T(2,128)S(1)}, s32[4,512]{1,0:T(4,128)S(1)}, s32[2048]{0:T(1024)S(1)}, /*i...) while((s32[]{:T(128)}, bf16[4,512,144]{1,2,0:T(8,128)(2,1)}, ...), condition=%wide.region_6.6_spmd, body=%wide.region_3.5_spmd.sunk | while | flops 630266880 | bytes 31176820 | solution.py:68
  329.0 38.9 %while.57 = (s32[]{:T(128)}, bf16[4,512,144]{1,2,0:T(8,128)(2,1)}, f32[4,2,512]{2,1,0:T(2,128)S(1)}, s32[4,512]{1,0:T(4,128)S(1)}, s32[2048]{0:T(1024)S(1)}, /*i...) while((s32[]{:T(128)}, bf16[4,512,144]{1,2,0:T(8,128)(2,1)}, ...), condition=%wide.region_6.6_spmd, body=%wide.region_3.5_spmd.sunk | while | flops 630266880 | bytes 31176820 | solution.py:68
  375.9 38.9 %while.57 = (s32[]{:T(128)}, bf16[4,512,144]{1,2,0:T(8,128)(2,1)}, f32[4,2,512]{2,1,0:T(2,128)S(1)}, s32[4,512]{1,0:T(4,128)S(1)}, s32[2048]{0:T(1024)S(1)}, /*i...) while((s32[]{:T(128)}, bf16[4,512,144]{1,2,0:T(8,128)(2,1)}, ...), condition=%wide.region_6.6_spmd, body=%wide.region_3.5_spmd.sunk | while | flops 630266880 | bytes 31176820 | solution.py:68
  434.0 446.0 %reduce-scatter.8.cloned.1.call-done = f32[768,1152]{1,0:T(8,128)} async-done(((f32[6144,1152]{1,0:T(8,128)}), f32[768,1152]{1,0:T(8,128)}) %reduce-scatter.8.cloned.1.call-update) | async-done | bytes 3538960 | tf_op jit(solution)/shard_map/reduce_scatter | solution.py:217
  896.1 189.6 %all-gather.8.cloned.1.call-done = bf16[6144,1152]{1,0:T(8,128)(2,1)} async-done(((bf16[768,1152]{1,0:T(8,128)(2,1)}), bf16[6144,1152]{1,0:T(8,128)(2,1)}) %all-gather.8.cloned.1.call-update) | async-done | bytes 14155792 | tf_op jit(solution)/shard_map/all_gather | solution.py:228
  1101.8 20.9 convolution_convert_fusion.1
  1122.8 159.1 %all-gather.10.cloned.1.call-done = bf16[6144,1152]{1,0:T(8,128)(2,1)} async-done(((bf16[768,1152]{1,0:T(8,128)(2,1)}), bf16[6144,1152]{1,0:T(8,128)(2,1)}) %all-gather.10.cloned.1.call-update) | async-done | bytes 14155792 | tf_op jit(solution)/shard_map/all_gather | solution.py:238
  1281.9 24.2 fusion.78
  1306.1 20.2 fusion.87
  1327.0 185.9 %reduce-scatter.10.cloned.1.call-done = bf16[768,1152]{1,0:T(8,128)(2,1)} async-done(((bf16[6144,1152]{1,0:T(8,128)(2,1)}), bf16[768,1152]{1,0:T(8,128)(2,1)}) %reduce-scatter.10.cloned.1.call-update) | async-done | bytes 1769488 | tf_op jit(solution)/shard_map/reduce_scatter | solution.py:232
  1512.9 451.3 %reduce-scatter.12.cloned.1.call-done = f32[768,1152]{1,0:T(8,128)} async-done(((f32[6144,1152]{1,0:T(8,128)}), f32[768,1152]{1,0:T(8,128)}) %reduce-scatter.12.cloned.1.call-update) | async-done | bytes 3538960 | tf_op jit(solution)/shard_map/reduce_scatter | solution.py:244
  1979.3 194.5 %all-gather.12.cloned.1.call-done = bf16[6144,1152]{1,0:T(8,128)(2,1)} async-done(((bf16[768,1152]{1,0:T(8,128)(2,1)}), bf16[6144,1152]{1,0:T(8,128)(2,1)}) %all-gather.12.cloned.1.call-update) | async-done | bytes 14155792 | tf_op jit(solution)/shard_map/all_gather | solution.py:253
  2186.6 265.0 %while.56 = (s32[]{:T(128)}, bf16[3,2048,144]{2,1,0:T(8,128)(2,1)}, bf16[3,2048,144]{1,2,0:T(8,128)(2,1)}, bf16[3,2048,144]{1,2,0:T(8,128)(2,1)}, bf16[3,2048,14...) while((s32[]{:T(128)}, bf16[3,2048,144]{2,1,0:T(8,128)(2,1)}, ...), condition=%wide.region_19.20_spmd, body=%wide.region_15.19_spmd.sunk | while | flops 1544666112 | bytes 114133608 | solution.py:152
  2204.9 63.7 %while.58 = (s32[]{:T(128)}, f32[2048,2,72]{0,2,1:T(8,128)}, f32[2048,2,72]{0,2,1:T(8,128)}, bf16[4,512,144]{1,2,0:T(8,128)(2,1)}, bf16[4,512,2,72]{1,3,2,0:T(8,...) while((s32[]{:T(128)}, f32[2048,2,72]{0,2,1:T(8,128)}, ...), condition=%wide.region_18.18_spmd.clone, body=%wide.region_16.17_spmd.clone.sunk | while | flops 1544076288 | bytes 95906112 | solution.py:115
  2293.0 63.8 %while.58 = (s32[]{:T(128)}, f32[2048,2,72]{0,2,1:T(8,128)}, f32[2048,2,72]{0,2,1:T(8,128)}, bf16[4,512,144]{1,2,0:T(8,128)(2,1)}, bf16[4,512,2,72]{1,3,2,0:T(8,...) while((s32[]{:T(128)}, f32[2048,2,72]{0,2,1:T(8,128)}, ...), condition=%wide.region_18.18_spmd.clone, body=%wide.region_16.17_spmd.clone.sunk | while | flops 1544076288 | bytes 95906112 | solution.py:115
  2381.2 63.8 %while.58 = (s32[]{:T(128)}, f32[2048,2,72]{0,2,1:T(8,128)}, f32[2048,2,72]{0,2,1:T(8,128)}, bf16[4,512,144]{1,2,0:T(8,128)(2,1)}, bf16[4,512,2,72]{1,3,2,0:T(8,...) while((s32[]{:T(128)}, f32[2048,2,72]{0,2,1:T(8,128)}, ...), condition=%wide.region_18.18_spmd.clone, body=%wide.region_16.17_spmd.clone.sunk | while | flops 1544076288 | bytes 95906112 | solution.py:115
  2487.9 20.8 convolution_convert_fusion.6
  2519.4 181.3 %reduce-scatter.14.cloned.1.call-done = bf16[768,1152]{1,0:T(8,128)(2,1)} async-done(((bf16[6144,1152]{1,0:T(8,128)(2,1)}), bf16[768,1152]{1,0:T(8,128)(2,1)}) %reduce-scatter.14.cloned.1.call-update) | async-done | bytes 1769488 | tf_op jit(solution)/shard_map/reduce_scatter | solution.py:271
  2735.3 56.6 %reduce-scatter.16.cloned.1.call-done = bf16[864,24]{1,0:T(8,128)(2,1)} async-done(((bf16[6912,24]{1,0:T(8,128)(2,1)}), bf16[864,24]{1,0:T(8,128)(2,1)}) %reduce-scatter.16.cloned.1.call-update) | async-done | bytes 41488
  2800.0 35.2 %all-reduce = (bf16[24,1152]{1,0:T(8,128)(2,1)S(1)}, bf16[1152]{0:T(1024)(128)(2,1)S(1)}, bf16[1152]{0:T(1024)(128)(2,1)S(1)}) all-reduce(bf16[24,1152]{1,0:T(8,128)(2,1)S(1)} %convolution_convert_fusion.9, bf16[1152]{0:T(1024)(128)(2,1)S(1)} %copy-done.49, bf16[1152]{0:T(1024)(128)(2,1)S(1)} %copy-done.48), channel_id=1, replica_groups=mesh['dp'=4,'head'=8] {'head'}, use_global_device_ids=true, to_apply=%region_24.25 | all-reduce | flops 29952 | bytes 119808 | tf_op jit(solution)/shard_map/psum | solution.py:307
  2850.8 58.7 %all-reduce.5.cloned.1.call-done = (bf16[1152,864]{0,1:T(8,128)(2,1)}, bf16[1152,3,144]{0,2,1:T(8,128)(2,1)}, bf16[144,1152]{1,0:T(8,128)(2,1)}, bf16[1152,576]{0,1:T(8,128)(2,1)}, bf16[576,1152]{1,0:T(8,128)(2,1)}) async-done(((bf16[1152,864]{0,1:T(8,128)(2,1)}, bf16[1152,3,144]{0,2,1:T(8,128)(2,1)}, bf16[144,1152]{1,0:T(8,128)(2,1)}, bf16[1152,576]{0,1:T(8,128)(2,1)}, bf16[576,1152]{1,0:T(8,128)(2,1)}), ...) | async-done | bytes 5971984 | tf_op jit(solution)/shard_map/psum | solution.py:313
  (628 shorter events, 636.1 us)
Async XLA Ops:
  7.2 253.7 %all-gather.6.cloned.1.call-start = ((), (), s32[]{:S(2)}) async-start(), calls=%async_computation.5 | async-start | bytes 15925248 | tf_op jit(solution)/shard_map/all_gather | solution.py:205
  9.9 45.5 %copy-start.37 = (f32[768]{0:T(1024)}, f32[768]{0:T(1024)S(1)}, u32[]{:S(2)}) copy-start(f32[768]{0:T(1024)S(1)} %broadcast_multiply_fusion.5) | copy-start | bytes 9220
  9.9 36.8 %copy-start.47 = (s32[6144]{0:T(1024)S(1)}, s32[6144]{0:T(1024)}, u32[]{:S(2)}) copy-start(s32[6144]{0:T(1024)} %param.23) | copy-start | bytes 73732
  12.0 43.4 %copy-start.45 = (f32[768]{0:T(1024)}, f32[768]{0:T(1024)S(1)}, u32[]{:S(2)}) copy-start(f32[768]{0:T(1024)S(1)} %add_rsqrt_fusion.1) | copy-start | bytes 9220
  62.4 198.5 %copy-start.58 = (bf16[1152,3,144]{0,2,1:T(8,128)(2,1)S(1)}, bf16[1152,3,144]{0,2,1:T(8,128)(2,1)}, u32[]{:S(2)}) copy-start(bf16[1152,3,144]{0,2,1:T(8,128)(2,1)} %param.27) | copy-start | bytes 2985988
  64.5 815.6 %reduce-scatter.8.cloned.1.call-start = ((), (), s32[]{:S(2)}) async-start(), calls=%async_computation.6 | async-start | bytes 31850496 | tf_op jit(solution)/shard_map/reduce_scatter | solution.py:217
  433.4 652.3 %all-gather.8.cloned.1.call-start = ((), (), s32[]{:S(2)}) async-start(), calls=%async_computation.7 | async-start | bytes 15925248 | tf_op jit(solution)/shard_map/all_gather | solution.py:228
  434.0 450.3 %copy-start.41 = (f32[1152]{0:T(1024)}, f32[1152]{0:T(1024)S(1)}, u32[]{:S(2)}) copy-start(f32[1152]{0:T(1024)S(1)} %convert_element_type.224) | copy-start | bytes 13828
  884.3 1087.7 %copy-start.35 = (f32[768]{0:T(1024)}, f32[768]{0:T(1024)S(1)}, u32[]{:S(2)}) copy-start(f32[768]{0:T(1024)S(1)} %broadcast_multiply_fusion.4) | copy-start | bytes 9220
  886.1 1085.9 %copy-start.39 = (f32[768]{0:T(1024)}, f32[768]{0:T(1024)S(1)}, u32[]{:S(2)}) copy-start(f32[768]{0:T(1024)S(1)} %add_rsqrt_fusion) | copy-start | bytes 9220
  891.2 390.6 %all-gather.10.cloned.1.call-start = ((), (), s32[]{:S(2)}) async-start(), calls=%async_computation.9 | async-start | bytes 15925248 | tf_op jit(solution)/shard_map/all_gather | solution.py:238
  896.1 616.9 %reduce-scatter.10.cloned.1.call-start = ((), (), s32[]{:S(2)}) async-start(), calls=%async_computation.8 | async-start | bytes 15925248 | tf_op jit(solution)/shard_map/reduce_scatter | solution.py:232
  896.1 385.7 %copy-start.52 = (f32[576]{0:T(1024)}, f32[576]{0:T(1024)S(1)}, u32[]{:S(2)}) copy-start(f32[576]{0:T(1024)S(1)} %convert_element_type.226) | copy-start | bytes 6916
  1122.7 841.5 %reduce-scatter.12.cloned.1.call-start = ((), (), s32[]{:S(2)}) async-start(), calls=%async_computation.10 | async-start | bytes 31850496 | tf_op jit(solution)/shard_map/reduce_scatter | solution.py:244
  1326.3 847.4 %all-gather.12.cloned.1.call-start = ((), (), s32[]{:S(2)}) async-start(), calls=%async_computation.11 | async-start | bytes 15925248 | tf_op jit(solution)/shard_map/all_gather | solution.py:253
  1327.0 645.0 %copy-start.43 = (f32[1152]{0:T(1024)}, f32[1152]{0:T(1024)S(1)}, u32[]{:S(2)}) copy-start(f32[1152]{0:T(1024)S(1)} %convert_element_type.230) | copy-start | bytes 13828
  1973.0 200.7 %copy-start.32 = (bf16[144,1152]{1,0:T(8,128)(2,1)S(1)}, bf16[144,1152]{1,0:T(8,128)(2,1)}, u32[]{:S(2)}) copy-start(bf16[144,1152]{1,0:T(8,128)(2,1)} %param.29) | copy-start | bytes 995332
  1979.2 721.5 %reduce-scatter.14.cloned.1.call-start = ((), (), s32[]{:S(2)}) async-start(), calls=%async_computation.12 | async-start | bytes 15925248 | tf_op jit(solution)/shard_map/reduce_scatter | solution.py:271
  2473.0 318.9 %reduce-scatter.16.cloned.1.call-start = ((), (), s32[]{:S(2)}) async-start(), calls=%async_computation.13 | async-start | bytes 1990656
  2519.4 183.2 %copy-start.38 = (f32[768]{0:T(1024)S(1)}, f32[768]{0:T(1024)}, u32[]{:S(2)}) copy-start(f32[768]{0:T(1024)} %copy-done.37) | copy-start | bytes 9220
  2519.4 183.2 %copy-start.46 = (f32[768]{0:T(1024)S(1)}, f32[768]{0:T(1024)}, u32[]{:S(2)}) copy-start(f32[768]{0:T(1024)} %copy-done.45) | copy-start | bytes 9220
  2726.0 65.9 %copy-start.30 = (f32[24,1152]{1,0:T(8,128)S(1)}, f32[24,1152]{1,0:T(8,128)}, u32[]{:S(2)}) copy-start(f32[24,1152]{1,0:T(8,128)} %param.24) | copy-start | bytes 331780
  2726.0 183.5 %all-reduce.5.cloned.1.call-start = ((), (), s32[]{:S(2)}) async-start(), calls=%async_computation.14 | async-start | bytes 11943936 | tf_op jit(solution)/shard_map/psum | solution.py:313
  2794.9 40.5 %copy-start.56 = (bf16[576]{0:T(1024)(128)(2,1)S(1)}, bf16[576]{0:T(1024)(128)(2,1)}, u32[]{:S(2)}) copy-start(bf16[576]{0:T(1024)(128)(2,1)} %get-tuple-element.468) | copy-start | bytes 3460
  (101 other events, 384.8 us)
Sparse Core Ops, SparseCore 0:
  64.6 196.2 all-gather.5
  433.5 446.5 reduce-scatter.7
  891.3 194.3 all-gather.7
  1088.3 193.4 all-gather.9
  1285.3 227.5 reduce-scatter.9
  1516.7 447.4 reduce-scatter.11
  1979.3 194.3 all-gather.11
  2473.2 227.5 reduce-scatter.13
  2726.1 65.7 reduce-scatter.15
  2795.6 113.8 all-reduce.4
where the time goes:
time: 2940 us; the launch traced here: 2930 us
  waiting for transfers between devices  2120 us (72%)
  matrix products  411 us (14%)
  other arithmetic  152 us (5%)
  local copies, waits for them, and re-layouts  147 us (5%)
  blocking collectives  80.5 us (3%)
    reduce_scatter x1, waiting for transfers between devices, local(): lax.psum_scatter(jnp.einsum('tf,df->td', grad_pre, w_fc1, preferred_eleme...  451 us
    reduce_scatter x1, waiting for transfers between devices, local(): lax.psum_scatter(jnp.dot(attn_mix, w_proj, preferred_element_type=jnp.flo...  446 us
    all_gather x1, waiting for transfers between devices, local(): gathered_a = lax.all_gather(attn_in, 'head', axis=0, tiled=True)  196 us
    all_gather x1, waiting for transfers between devices, local(): grad_rows_a = lax.all_gather(grad_branch_a, 'head', axis=0, tiled=True)  194 us
    all_gather x1, waiting for transfers between devices, local(): gathered_m = lax.all_gather(mlp_in, 'head', axis=0, tiled=True)  190 us
    reduce_scatter x1, waiting for transfers between devices, local(): lax.psum_scatter(jnp.dot(hidden_low, w_fc2, preferred_element_type=jnp.fl...  186 us
    reduce_scatter x1, waiting for transfers between devices, local(): lax.psum_scatter(jnp.einsum('tc,dc->td', grad_qkv, qkv_weight, preferred_...  181 us
    all_gather x1, waiting for transfers between devices, local(): grad_rows_m = lax.all_gather(grad_branch_m, 'head', axis=0, tiled=True)  159 us
  transfers between devices with their start and end apart: 10, of which 10 were waited for; matrix products, arithmetic and copies ran while one was open for 5% of the time, Pallas kernels for 0%

commit v1 on v0

v1 whole, which is shorter than its diff:
```python
import functools
import math

import jax
import jax.numpy as jnp
from jax import lax
from jax.experimental import pallas as pl
from jax.experimental.pallas import tpu as pltpu
from jax.sharding import Mesh
from jax.sharding import PartitionSpec as P

HEAD_DIM = 72
LONG_SEQ = 1024
SHORT_SEQ = 256
LANES = 128
NORM_EPS = 1e-06
TOP = lax.Precision.HIGHEST
F32 = jnp.float32
BF16 = jnp.bfloat16

OUTER, CORE, PART, GROUP = "outer", "core", "part", "group"
DP = (OUTER, CORE)
HEAD = (PART, GROUP)
SPREAD = (CORE, PART, GROUP)
EVERY = (OUTER, CORE, PART, GROUP)

NT = (((1,), (1,)), ((), ()))
TN = (((0,), (0,)), ((), ()))


def layer_norm(values):
    centered = values - jnp.mean(values, axis=-1, keepdims=True)
    inverse = lax.rsqrt(jnp.mean(centered * centered, axis=-1, keepdims=True) + NORM_EPS)
    return (centered * inverse, inverse)


def norm_back(grad_normed, normed, inverse):
    mean_grad = jnp.mean(grad_normed, axis=-1, keepdims=True)
    mean_cross = jnp.mean(grad_normed * normed, axis=-1, keepdims=True)
    return inverse * (grad_normed - mean_grad - normed * mean_cross)


def head_columns(index, cols, offset):
    per_shard = cols // HEAD_DIM
    shard, within = index // per_shard, index % per_shard
    return shard * 3 * cols + offset * cols + within * HEAD_DIM


def attend_kernel(heads, cols, single_ref, qkv_ref, mix_ref, q_s, k_s, v_s, o_s):
    scale = 1.0 / math.sqrt(HEAD_DIM)
    units = LONG_SEQ // SHORT_SEQ
    pad = jnp.zeros((LONG_SEQ, LANES - HEAD_DIM), BF16)
    for h in range(heads):
        for offset, ref in enumerate((q_s, k_s, v_s)):
            at = head_columns(h, cols, offset)
            ref[h, :, :HEAD_DIM] = qkv_ref[:, at : at + HEAD_DIM]
            ref[h, :, HEAD_DIM:] = pad

    def attend_keys(h, rows, key_rows):
        scores = (
            lax.dot_general(q_s[h, rows], k_s[h, key_rows], NT, preferred_element_type=F32) * scale
        )
        weights = jnp.exp(scores - jnp.max(scores, axis=-1, keepdims=True))
        probs = weights * (1.0 / jnp.sum(weights, axis=-1, keepdims=True))
        o_s[h, rows] = jnp.dot(
            probs.astype(BF16), v_s[h, key_rows], preferred_element_type=F32
        ).astype(BF16)

    def step(i, carry):
        h = i // units
        rows = pl.ds(pl.multiple_of((i % units) * SHORT_SEQ, SHORT_SEQ), SHORT_SEQ)

        @pl.when(single_ref[pl.program_id(0)] == 1)
        def _():
            attend_keys(h, rows, slice(None))

        @pl.when(single_ref[pl.program_id(0)] == 0)
        def _():
            attend_keys(h, rows, rows)

        return carry

    lax.fori_loop(0, heads * units, step, 0)
    for h in range(heads):
        mix_ref[:, h * HEAD_DIM : (h + 1) * HEAD_DIM] = o_s[h, :, :HEAD_DIM]


def attend(single, qkv, heads, cols):
    rows, width = qkv.shape
    blocks = rows // LONG_SEQ
    return pl.pallas_call(
        functools.partial(attend_kernel, heads, cols),
        grid_spec=pltpu.PrefetchScalarGridSpec(
            num_scalar_prefetch=1,
            grid=(blocks,),
            in_specs=[pl.BlockSpec((LONG_SEQ, width), lambda b, s: (b, 0))],
            out_specs=pl.BlockSpec((LONG_SEQ, heads * HEAD_DIM), lambda b, s: (b, 0)),
            scratch_shapes=[pltpu.VMEM((heads, LONG_SEQ, LANES), BF16)] * 4,
        ),
        out_shape=jax.ShapeDtypeStruct((rows, heads * HEAD_DIM), BF16),
        cost_estimate=pl.CostEstimate(
            flops=4 * rows * LONG_SEQ * heads * LANES,
            bytes_accessed=2 * rows * (width + heads * HEAD_DIM),
            transcendentals=rows * LONG_SEQ * heads,
        ),
        name="attend",
    )(single, qkv)


def attend_back_kernel(
    heads, cols, single_ref, qkv_ref, grad_ref, out_ref, q_s, k_s, v_s, g_s, dq_s, dk_s, dv_s, kt_s
):
    scale = 1.0 / math.sqrt(HEAD_DIM)
    units = LONG_SEQ // SHORT_SEQ
    pad = jnp.zeros((LONG_SEQ, LANES - HEAD_DIM), BF16)
    for h in range(heads):
        for offset, ref in enumerate((q_s, k_s, v_s)):
            at = head_columns(h, cols, offset)
            ref[h, :, :HEAD_DIM] = qkv_ref[:, at : at + HEAD_DIM]
            ref[h, :, HEAD_DIM:] = pad
        g_s[h, :, :HEAD_DIM] = grad_ref[:, h * HEAD_DIM : (h + 1) * HEAD_DIM]
        g_s[h, :, HEAD_DIM:] = pad
        kt_s[h] = k_s[h].T
    is_single = single_ref[pl.program_id(0)] == 1

    def grads(h, rows, key_rows):
        q, g = q_s[h, rows], g_s[h, rows]
        k, v = k_s[h, key_rows], v_s[h, key_rows]
        scores = lax.dot_general(k, q, NT, preferred_element_type=F32) * scale
        weights = jnp.exp(scores - jnp.max(scores, axis=0, keepdims=True))
        probs = weights * (1.0 / jnp.sum(weights, axis=0, keepdims=True))
        grad_probs = lax.dot_general(v, g, NT, preferred_element_type=F32)
        inner = jnp.sum(probs * grad_probs, axis=0, keepdims=True)
        grad_scores = (probs * (grad_probs - inner)).astype(BF16)
        grad_v = jnp.dot(probs.astype(BF16), g, preferred_element_type=F32)
        grad_k = jnp.dot(grad_scores, q, preferred_element_type=F32)
        grad_q = jnp.dot(kt_s[h, :, key_rows], grad_scores, preferred_element_type=F32)
        dq_s[h, rows] = (grad_q.T * scale).astype(BF16)
        return grad_k, grad_v

    @pl.when(is_single)
    def _():
        dk_s[...] = jnp.zeros_like(dk_s)
        dv_s[...] = jnp.zeros_like(dv_s)

    def step(i, carry):
        h = i // units
        rows = pl.ds(pl.multiple_of((i % units) * SHORT_SEQ, SHORT_SEQ), SHORT_SEQ)

        @pl.when(is_single)
        def _():
            grad_k, grad_v = grads(h, rows, slice(None))
            dk_s[h] += grad_k
            dv_s[h] += grad_v

        @pl.when(jnp.logical_not(is_single))
        def _():
            grad_k, grad_v = grads(h, rows, rows)
            dk_s[h, rows] = grad_k
            dv_s[h, rows] = grad_v

        return carry

    lax.fori_loop(0, heads * units, step, 0)
    for h in range(heads):
        for offset, value in enumerate(
            (dq_s[h], (dk_s[h] * scale).astype(BF16), dv_s[h].astype(BF16))
        ):
            at = head_columns(h, cols, offset)
            out_ref[:, at : at + HEAD_DIM] = value[:, :HEAD_DIM]


def attend_back(single, qkv, grad_mix, heads, cols):
    rows, width = qkv.shape
    blocks = rows // LONG_SEQ
    low = pltpu.VMEM((heads, LONG_SEQ, LANES), BF16)
    wide = pltpu.VMEM((heads, LONG_SEQ, LANES), F32)
    return pl.pallas_call(
        functools.partial(attend_back_kernel, heads, cols),
        grid_spec=pltpu.PrefetchScalarGridSpec(
            num_scalar_prefetch=1,
            grid=(blocks,),
            in_specs=[
                pl.BlockSpec((LONG_SEQ, width), lambda b, s: (b, 0)),
                pl.BlockSpec((LONG_SEQ, heads * HEAD_DIM), lambda b, s: (b, 0)),
            ],
            out_specs=pl.BlockSpec((LONG_SEQ, width), lambda b, s: (b, 0)),
            scratch_shapes=[low] * 5 + [wide] * 2 + [pltpu.VMEM((heads, LANES, LONG_SEQ), BF16)],
        ),
        out_shape=jax.ShapeDtypeStruct((rows, width), BF16),
        cost_estimate=pl.CostEstimate(
            flops=10 * rows * LONG_SEQ * heads * LANES,
            bytes_accessed=2 * rows * (2 * width + heads * HEAD_DIM),
            transcendentals=rows * LONG_SEQ * heads,
        ),
        name="attend_back",
    )(single, qkv, grad_mix)


def mlp_kernel(x_ref, g_ref, w1_ref, w2_ref, b1_ref, out_ref, gin_ref, d1_ref, d2_ref, db_ref):
    @pl.when(pl.program_id(0) == 0)
    def _():
        out_ref[...] = jnp.zeros_like(out_ref)
        gin_ref[...] = jnp.zeros_like(gin_ref)

    root = math.sqrt(2.0 / math.pi)
    x, g, w1, w2 = x_ref[...], g_ref[...], w1_ref[...], w2_ref[...]
    pre = lax.dot_general(x, w1, NT, preferred_element_type=F32) + b1_ref[0]
    grad_hidden = lax.dot_general(g, w2, NT, preferred_element_type=F32)
    square = pre * pre
    bent = jnp.tanh(root * (pre * (1.0 + 0.044715 * square)))
    half = 0.5 * (1.0 + bent)
    slope = half + (0.5 * root) * pre * (1.0 - bent * bent) * (1.0 + (3 * 0.044715) * square)
    hidden = (pre * half).astype(BF16)
    grad_pre = (grad_hidden * slope).astype(BF16)
    out_ref[...] += jnp.dot(hidden, w2, preferred_element_type=F32)
    gin_ref[...] += jnp.dot(grad_pre, w1, preferred_element_type=F32)
    d2_ref[...] = lax.dot_general(hidden, g, TN, preferred_element_type=F32).astype(BF16)
    d1_ref[...] = lax.dot_general(grad_pre, x, TN, preferred_element_type=F32).astype(BF16)
    db_ref[0] = jnp.sum(grad_pre.astype(F32), axis=0, keepdims=True)


def mlp(x, g, w1, w2, b1):
    rows, width = x.shape
    units = w1.shape[0]
    tile = next(t for t in (512, 256, 128) if units % t == 0)
    tiles = units // tile
    whole = pl.BlockSpec((rows, width), lambda f: (0, 0))
    piece = pl.BlockSpec((tile, width), lambda f: (f, 0))
    line = pl.BlockSpec((1, 1, tile), lambda f: (f, 0, 0))
    return pl.pallas_call(
        mlp_kernel,
        grid=(tiles,),
        in_specs=[whole, whole, piece, piece, line],
        out_specs=[whole, whole, piece, piece, line],
        out_shape=[
            jax.ShapeDtypeStruct((rows, width), F32),
            jax.ShapeDtypeStruct((rows, width), F32),
            jax.ShapeDtypeStruct((units, width), BF16),
            jax.ShapeDtypeStruct((units, width), BF16),
            jax.ShapeDtypeStruct((tiles, 1, tile), F32),
        ],
        cost_estimate=pl.CostEstimate(
            flops=12 * rows * width * units,
            bytes_accessed=8 * units * width + 12 * rows * width,
            transcendentals=rows * units,
        ),
        name="mlp",
    )(x, g, w1, w2, b1.reshape(tiles, 1, tile))


def xor_pairs(size, mask):
    return [(i, i ^ mask) for i in range(size)]


def swap(value, axis, size, mask):
    return lax.ppermute(value, axis, xor_pairs(size, mask))


def gather_group(own, size):
    rows = own.shape[0]
    me = lax.axis_index(GROUP)
    if size != 4:
        return lax.all_gather(own, GROUP, axis=0, tiled=True)
    half = rows // 2
    near = swap(own, GROUP, 4, 1)
    far = swap(own, GROUP, 4, 2)
    upper = swap(far[:half], GROUP, 4, 1)
    lower = swap(near[half:], GROUP, 4, 2)
    whole = jnp.zeros((4 * rows, own.shape[1]), own.dtype)
    for mask, at, piece in (
        (0, 0, own),
        (1, 0, near),
        (2, 0, far),
        (3, 0, upper),
        (3, half, lower),
    ):
        start = jnp.bitwise_xor(me, mask) * rows + at
        whole = lax.dynamic_update_slice_in_dim(whole, piece, start, 0)
    return whole


def scatter_group(partial, size):
    if size != 4:
        return lax.psum_scatter(partial, GROUP, scatter_dimension=0, tiled=True).astype(F32)
    rows = partial.shape[0] // 4
    half = rows // 2
    me = lax.axis_index(GROUP)

    def piece(mask, at):
        start = jnp.bitwise_xor(me, mask) * rows + at
        return lax.dynamic_slice_in_dim(partial, start, half)

    upper = swap(jnp.stack([piece(1, 0), piece(3, 0)]), GROUP, 4, 1)
    lower = swap(jnp.stack([piece(2, half), piece(3, half)]), GROUP, 4, 2)
    upper_far = swap((piece(2, 0).astype(F32) + upper[1].astype(F32)).astype(BF16), GROUP, 4, 2)
    lower_far = swap((piece(1, half).astype(F32) + lower[1].astype(F32)).astype(BF16), GROUP, 4, 1)
    return jnp.concatenate(
        [
            piece(0, 0).astype(F32) + upper[0].astype(F32) + upper_far.astype(F32),
            piece(0, half).astype(F32) + lower[0].astype(F32) + lower_far.astype(F32),
        ]
    )


def sum_outer(value, size):
    total = value.astype(F32)
    if size & (size - 1):
        return lax.psum(value, OUTER).astype(F32)
    mask = 1
    while mask < size:
        total = total + swap(total.astype(BF16), OUTER, size, mask).astype(F32)
        total = total if mask * 2 >= size else total.astype(BF16).astype(F32)
        mask *= 2
    return total


def join_cores(own):
    own = own.astype(BF16)
    other = swap(own, CORE, 2, 1)
    first = lax.axis_index(CORE) == 0
    return jnp.concatenate([jnp.where(first, own, other), jnp.where(first, other, own)])


def core_half(value):
    half = value.shape[0] // 2
    return lax.dynamic_slice_in_dim(value, lax.axis_index(CORE) * half, half)


def local(
    sizes,
    tokens,
    segment_ids,
    cond,
    w_ada,
    b_ada,
    w_qkv,
    bias_qv,
    w_proj,
    b_proj,
    w_fc1,
    b_fc1,
    w_fc2,
    b_fc2,
    cotangent,
):
    outer_size, part_size, group_size = sizes
    head_size = part_size * group_size
    rows, width = tokens.shape
    slots = cond.shape[0]
    cols = w_qkv.shape[2]
    ada_cols = w_ada.shape[1]
    ff_here = w_fc1.shape[1]
    unit = math.gcd(rows, SHORT_SEQ)
    units = rows // unit
    heads = part_size * cols // HEAD_DIM
    head_at = lax.axis_index(HEAD)

    proj_half, fc1_half = cols // 2, ff_here // 2
    bias_row = jnp.pad(core_half(b_fc1)[None, :], ((0, 0), (0, width - fc1_half)))
    proj_sent = jnp.concatenate([core_half(w_proj), bias_row])
    proj_rows = lax.all_gather(proj_sent, SPREAD, axis=0)
    proj_rows = proj_rows.reshape(2 * head_size, proj_half + 1, width)
    proj_full = proj_rows[:, :proj_half].reshape(-1, width)
    bias_fc1 = proj_rows[:, proj_half, :fc1_half].reshape(-1).astype(F32)
    fc1_full = lax.all_gather(core_half(w_fc1.T), SPREAD, axis=0, tiled=True)
    fc2_full = lax.all_gather(core_half(w_fc2), SPREAD, axis=0, tiled=True)
    qkv_own = jnp.transpose(w_qkv, (1, 2, 0)).reshape(3 * cols, width)
    if part_size == 2:
        qkv_other = swap(qkv_own, PART, 2, 1)
        low_part = lax.axis_index(PART) == 0
        qkv_weight = jnp.concatenate(
            [jnp.where(low_part, qkv_own, qkv_other), jnp.where(low_part, qkv_other, qkv_own)]
        )
    else:
        qkv_weight = lax.all_gather(qkv_own, PART, axis=0, tiled=True)
    bias_own = jnp.concatenate([bias_qv[0], jnp.zeros((cols,), bias_qv.dtype), bias_qv[1]])
    qkv_bias = lax.all_gather(bias_own, PART, axis=0, tiled=True).astype(F32)

    unit_ids = segment_ids[::unit] - lax.axis_index(DP) * slots
    pick = (unit_ids[:, None] == jnp.arange(slots, dtype=jnp.int32)[None, :]).astype(F32)
    cond_act, silu_back = jax.vjp(jax.nn.silu, cond)
    cond_low = cond_act.astype(BF16)
    cond_all = lax.all_gather(cond_low, DP, axis=0, tiled=True)
    mod_part = jnp.dot(cond_low, w_ada, preferred_element_type=F32) + b_ada.astype(F32)
    mod_sent = jnp.dot(pick, mod_part, precision=TOP).reshape(head_size, units, ada_cols)
    mod_got = lax.all_to_all(mod_sent, HEAD, split_axis=0, concat_axis=0, tiled=True)
    modulation = jnp.transpose(mod_got, (1, 0, 2)).reshape(units, 6, 1, width)
    shift_a, scale_a, gate_a, shift_m, scale_m, gate_m = [modulation[:, i] for i in range(6)]

    def by_unit(value):
        return value.reshape(units, unit, width)

    def flat(value):
        return value.reshape(rows, width)

    resid = by_unit(tokens.astype(F32))
    normed_a, inverse_a = layer_norm(resid)
    attn_in = flat((normed_a * (1.0 + scale_a) + shift_a).astype(BF16))
    gathered = gather_group(attn_in, group_size)
    qkv = (lax.dot_general(gathered, qkv_weight, NT, preferred_element_type=F32) + qkv_bias).astype(
        BF16
    )
    blocks = gathered.shape[0] // LONG_SEQ
    first = lax.axis_index(PART) * gathered.shape[0] + jnp.arange(blocks) * LONG_SEQ
    single = (segment_ids[first] == segment_ids[first + SHORT_SEQ]).astype(jnp.int32)
    mix_part = attend(single, qkv, heads, cols)
    mix_got = lax.all_to_all(
        mix_part.reshape(group_size, rows, heads * HEAD_DIM), GROUP, split_axis=0, concat_axis=0
    )
    mix_got = mix_got.reshape(group_size, rows, part_size, 2, proj_half)
    mix = jnp.transpose(mix_got, (1, 3, 2, 0, 4)).reshape(rows, width)
    branch_a = by_unit(
        jnp.dot(mix, proj_full, preferred_element_type=F32) + b_proj.astype(F32)
    )
    mid = resid + gate_a * branch_a
    normed_m, inverse_m = layer_norm(mid)
    mlp_in = flat((normed_m * (1.0 + scale_m) + shift_m).astype(BF16))
    cotan = by_unit(cotangent.astype(F32))
    grad_branch_m = flat((gate_m * cotan).astype(BF16))
    branch_m, grad_mlp_in, grad_fc1, grad_fc2, grad_b1 = mlp(
        mlp_in, grad_branch_m, fc1_full, fc2_full, bias_fc1
    )
    grad_fc2 = lax.psum_scatter(grad_fc2, SPREAD, scatter_dimension=0, tiled=True)
    grad_fc1 = lax.psum_scatter(grad_fc1, SPREAD, scatter_dimension=0, tiled=True)
    branch_m = by_unit(branch_m) + b_fc2.astype(F32)
    grad_mlp_in = by_unit(grad_mlp_in)
    output = flat((mid + gate_m * branch_m).astype(BF16))
    grad_mid = cotan + norm_back(grad_mlp_in * (1.0 + scale_m), normed_m, inverse_m)
    grad_branch_a = flat((gate_a * grad_mid).astype(BF16))
    grad_mix = lax.dot_general(grad_branch_a, proj_full, NT, preferred_element_type=F32)
    grad_mix = grad_mix.astype(BF16).reshape(rows, 2, part_size, group_size, proj_half)
    grad_mix = jnp.transpose(grad_mix, (3, 0, 2, 1, 4)).reshape(group_size, rows, -1)
    grad_mix = lax.all_to_all(grad_mix, GROUP, split_axis=0, concat_axis=0)
    grad_proj = lax.dot_general(mix, grad_branch_a, TN, preferred_element_type=F32).astype(BF16)
    b1_row = jnp.pad(
        grad_b1.reshape(2 * head_size, 1, fc1_half).astype(BF16),
        ((0, 0), (0, 0), (0, width - fc1_half)),
    )
    grad_proj = jnp.concatenate([grad_proj.reshape(2 * head_size, proj_half, width), b1_row], axis=1)
    grad_proj = lax.psum_scatter(grad_proj, SPREAD, scatter_dimension=0, tiled=True)[0]
    grad_qkv = attend_back(single, qkv, grad_mix.reshape(-1, heads * HEAD_DIM), heads, cols)
    attn_grad_part = jnp.dot(grad_qkv, qkv_weight, preferred_element_type=F32).astype(BF16)
    grad_attn_in = by_unit(scatter_group(attn_grad_part, group_size))

    grad_w_qkv = lax.dot_general(grad_qkv, gathered, TN, preferred_element_type=F32)
    grad_bias = jnp.sum(grad_qkv.astype(F32), axis=0)
    bias_rows = jnp.pad(grad_bias.reshape(part_size, 1, 3 * cols), ((0, 0), (0, 0), (0, width - 3 * cols)))
    pad_rows = jnp.zeros((part_size, 15, width), F32)
    grad_w_qkv = jnp.concatenate(
        [grad_w_qkv.reshape(part_size, 3 * cols, width), bias_rows, pad_rows], axis=1
    ).astype(BF16)
    if part_size == 2:
        mine, theirs = grad_w_qkv[0], grad_w_qkv[1]
        low_part = lax.axis_index(PART) == 0
        kept = jnp.where(low_part, mine, theirs)
        sent = jnp.where(low_part, theirs, mine)
        grad_w_qkv = kept.astype(F32) + swap(sent, PART, 2, 1).astype(F32)
    else:
        grad_w_qkv = lax.psum_scatter(
            grad_w_qkv, PART, scatter_dimension=0, tiled=True
        )[0].astype(F32)
    half = grad_w_qkv.shape[0] // 2
    other = swap(
        lax.dynamic_slice_in_dim(grad_w_qkv, (1 - lax.axis_index(CORE)) * half, half).astype(BF16),
        CORE,
        2,
        1,
    )
    grad_w_qkv = (core_half(grad_w_qkv) + other.astype(F32)).astype(BF16)
    grad_w_qkv = join_cores(sum_outer(grad_w_qkv, outer_size)).astype(F32)
    grad_bias = grad_w_qkv[3 * cols, : 3 * cols]
    grad_bias_qv = jnp.stack([grad_bias[:cols], grad_bias[2 * cols :]])
    grad_w_qkv = jnp.transpose(grad_w_qkv[: 3 * cols].reshape(3, cols, width), (2, 0, 1))

    grad_fc2 = join_cores(sum_outer(grad_fc2, outer_size)).astype(F32)
    grad_fc1 = join_cores(sum_outer(grad_fc1, outer_size)).astype(F32).T
    grad_proj = join_cores(sum_outer(grad_proj, outer_size)).astype(F32)
    grad_proj = grad_proj.reshape(2, proj_half + 1, width)
    grad_b1 = grad_proj[:, proj_half, :fc1_half].reshape(-1)
    grad_proj = grad_proj[:, :proj_half].reshape(cols, width)

    grad_tokens = flat(
        (grad_mid + norm_back(grad_attn_in * (1.0 + scale_a), normed_a, inverse_a)).astype(BF16)
    )
    unit_grad = jnp.concatenate(
        [
            jnp.sum(value, axis=1)
            for value in (
                grad_attn_in,
                grad_attn_in * normed_a,
                grad_mid * branch_a,
                grad_mlp_in,
                grad_mlp_in * normed_m,
                cotan * branch_m,
            )
        ],
        axis=1,
    )
    unit_grad = jnp.transpose(unit_grad.reshape(units, head_size, ada_cols), (1, 0, 2))
    unit_grad = lax.all_to_all(unit_grad, HEAD, split_axis=0, concat_axis=0, tiled=True)
    grad_mod = lax.dot_general(
        pick, unit_grad.reshape(head_size * units, ada_cols), TN, precision=TOP
    )
    grad_mod_all = lax.all_gather(grad_mod, DP, axis=0, tiled=True)
    grad_w_ada = lax.dot_general(cond_all.astype(F32), grad_mod_all, TN, precision=TOP)
    grad_b_ada = jnp.sum(grad_mod_all, axis=0)
    grad_cond_part = lax.dot_general(grad_mod, w_ada.astype(F32), NT, precision=TOP)
    grad_cond = silu_back(lax.psum(grad_cond_part, HEAD))[0]
    bias_parts = jnp.stack(
        [
            jnp.sum(grad_branch_a.astype(F32), axis=0),
            jnp.sum(grad_branch_m.astype(F32), axis=0),
        ]
    )
    bias_sums = lax.psum(bias_parts, EVERY)
    return (
        output,
        grad_tokens,
        grad_cond,
        grad_w_ada,
        grad_b_ada,
        grad_w_qkv,
        grad_bias_qv,
        grad_proj,
        bias_sums[0],
        grad_fc1,
        grad_b1,
        grad_fc2,
        bias_sums[1],
    )


def solution(mesh):
    dp_size, head_size = mesh.shape["dp"], mesh.shape["head"]

    def run(*arrays):
        rows = arrays[0].shape[0] // (dp_size * head_size)
        group_size = math.lcm(rows, LONG_SEQ) // rows
        sizes = (dp_size // 2, head_size // group_size, group_size)
        finer = Mesh(
            mesh.devices.reshape(sizes[0], 2, sizes[1], sizes[2]), (OUTER, CORE, PART, GROUP)
        )
        placed = (
            P(EVERY, None),
            P(DP),
            P(DP, None),
            P(None, HEAD),
            P(HEAD),
            P(None, None, HEAD),
            P(None, HEAD),
            P(HEAD, None),
            P(),
            P(None, HEAD),
            P(HEAD),
            P(HEAD, None),
            P(),
            P(EVERY, None),
        )
        results = (
            P(EVERY, None),
            P(EVERY, None),
            P(DP, None),
            P(None, HEAD),
            P(HEAD),
            P(None, None, HEAD),
            P(None, HEAD),
            P(HEAD, None),
            P(),
            P(None, HEAD),
            P(HEAD),
            P(HEAD, None),
            P(),
        )
        return jax.shard_map(
            functools.partial(local, sizes),
            mesh=finer,
            in_specs=placed,
            out_specs=results,
            check_vma=False,
        )(*arrays)

    return run
```

time: 2940 us -> 904 us (0.31)
  waiting for transfers between devices: 2120 us -> 325 us
  matrix products: 411 us -> 52.9 us
  Pallas kernels: 0 us -> 165 us
  local copies, waits for them, and re-layouts: 147 us -> 60.9 us
  other arithmetic: 152 us -> 70.2 us
  blocking collectives: 80.5 us -> 158 us
  starting transfers between devices: 0.76 us -> 44.8 us
    reduce_scatter x4 -> x3, waiting for transfers between devices: 1260 us -> 0.02 us  [the longest x1 0.02 us: local(): lax.psum_scatter(grad_fc2, SPREAD, scatter_dimension=0, tiled=True)]
    all_gather x4 -> x3, waiting for transfers between devices: 739 us -> 6.3 us  [the longest x1 6.28 us: local(): fc2_full = lax.all_gather(core_half(w_fc2), SPREAD, axis=0, tiled=True)]
    dot_general x101 -> x11, matrix products: 411 us -> 52.9 us  [the longest x1 10.7 us: local(): lax.dot_general(grad_qkv, gathered, TN, preferred_element_type=F32)]
    ppermute x0 -> x19, waiting for transfers between devices: none -> 226 us  [swap(): return lax.ppermute(value, axis, xor_pairs(size, mask))]
    pallas_call x0 -> x3, Pallas kernels: none -> 165 us  [the longest x1 65.3 us: mlp(): pl.pallas_call(mlp_kernel, grid=(tiles,), in_specs=[whole, whole, piece,...]
    unnamed x0 -> x1, blocking collectives: none -> 80.1 us
    unnamed x11 -> x7, waiting for transfers between devices: 56.7 us -> 0.63 us
    convert_element_type x35 -> x19, other arithmetic: 60.7 us -> 19.3 us  [the longest x1 6 us: local(): (grad_mid + norm_back(grad_attn_in * (1.0 + scale_a), normed_a, inverse_a...]
  transfers between devices with their start and end apart: 10 -> 30, of which waited for: 10 -> 16; matrix products, arithmetic and copies ran while one was open for 5% -> 16% of each run, Pallas kernels for 0% -> 11%
where the time goes in v1:
time: 904 us; the launch traced here: 893 us
  waiting for transfers between devices  325 us (36%)
  Pallas kernels  165 us (18%)
  blocking collectives  158 us (17%)
  other arithmetic  70.2 us (8%)
  local copies, waits for them, and re-layouts  60.9 us (7%)
  matrix products  52.9 us (6%)
  starting transfers between devices  44.8 us (5%)
  between operations  16.2 us (2%)
    ppermute x19, waiting for transfers between devices, swap(): return lax.ppermute(value, axis, xor_pairs(size, mask))  226 us
    unnamed x1, blocking collectives  80.1 us
    pallas_call x1, Pallas kernels, mlp(): pl.pallas_call(mlp_kernel, grid=(tiles,), in_specs=[whole, whole, piece,...  65.3 us
    psum x1, waiting for transfers between devices, local(): grad_cond = silu_back(lax.psum(grad_cond_part, HEAD))[0]  64.1 us
    pallas_call x1, Pallas kernels, attend_back(): pl.pallas_call(functools.partial(attend_back_kernel, heads, cols), grid_s...  59.6 us
    psum x1, blocking collectives, local(): bias_sums = lax.psum(bias_parts, EVERY)  56.9 us
    pallas_call x1, Pallas kernels, attend(): pl.pallas_call(functools.partial(attend_kernel, heads, cols), grid_spec=p...  40.2 us
    ppermute x19, starting transfers between devices, swap(): return lax.ppermute(value, axis, xor_pairs(size, mask))  24.4 us
  transfers between devices with their start and end apart: 30, of which 16 were waited for; matrix products, arithmetic and copies ran while one was open for 16% of the time, Pallas kernels for 11%

profile of v1, /device:TPU:0, one launch (start us, length us, event | category | flops | bytes accessed | tf_op | source)
XLA Modules:
  0.0 893.3 jit_solution(4013877907800093393)
XLA Ops:
  15.8 7.3 all-to-all-start
  43.3 80.1 %all-reduce.3 = bf16[864]{0:T(1024)(128)(2,1)S(1)} all-reduce(bf16[864]{0:T(1024)(128)(2,1)S(1)} %dynamic-update-slice), channel_id=1, replica_groups=mesh['outer'=2,'core'=2,'part'=2,'group'=4] {'part'}, use_global_device_ids=true, to_apply=%add.3 | all-reduce | flops 864 | bytes 3456
  125.1 8.7 collective-permute-done.1
  142.5 21.3 %collective-permute-done.2 = bf16[384,1152]{1,0:T(8,128)(2,1)S(1)} collective-permute-done((bf16[384,1152]{1,0:T(8,128)(2,1)S(1)}, bf16[384,1152]{1,0:T(8,128)(2,1)S(1)}, u32[]{:S(2)}, u32[]{:S(2)}) %collective-permute-start.2) | collective-permute-done | bytes 884768 | tf_op jit(solution)/shard_map/ppermute | solution.py:257
  164.0 26.4 %collective-permute-done.3 = bf16[384,1152]{1,0:T(8,128)(2,1)S(1)} collective-permute-done((bf16[384,1152]{1,0:T(8,128)(2,1)S(1)}, bf16[384,1152]{1,0:T(8,128)(2,1)S(1)}, u32[]{:S(2)}, u32[]{:S(2)}) %collective-permute-start.3) | collective-permute-done | bytes 884768 | tf_op jit(solution)/shard_map/ppermute | solution.py:257
  193.3 9.8 %add_convert_fusion.qkv_ref = bf16[3072,864]{1,0:T(8,128)(2,1)} fusion(f32[864]{0:T(1024)S(1)} %convert_element_type.231, bf16[3072,1152]{1,0:T(8,128)(2,1)S(1)} %constant_dynamic-update-slice_fusion.6, bf16[432,1152]{1,0:T(8,128)(2,1)S(1)} %get-tuple-element.53, bf16[432,1152]{1,0:T(8,128)(2,1)S(1)} %get-tuple-element.52), kind=kOutput, calls=%fused_computation.3 | convolution fusion | flops 6124584960 | bytes 14380416 | tf_op jit(solution)/shard_map/dot_general | solution.py:401
  203.0 40.2 %attend.1 = bf16[3072,288]{1,0:T(8,128)(2,1)} custom-call(s32[3]{0:T(128)} %compare_convert_fusion.single_ref, bf16[3072,864]{1,0:T(8,128)(2,1)} %add_convert_fusion.qkv_ref), custom_call_target="tpu_custom_call" | custom-call | flops 6442450944 | bytes 7077888 | tf_op jit(solution)/shard_map/attend/pallas_call | solution.py:91
  260.5 21.9 %all-to-all-done.1 = bf16[4,768,288]{1,2,0:T(8,128)(2,1)} async-done(((bf16[4,768,288]{1,2,0:T(8,128)(2,1)}), bf16[4,768,288]{1,2,0:T(8,128)(2,1)}, u32[]{:S(2)}, u32[]{:S(2)}) %all-to-all-start.1) | async-done | bytes 1769504 | tf_op jit(solution)/shard_map/all_to_all | solution.py:408
  284.8 6.9 fusion.36
  295.6 6.3 all-gather.8.cloned.1.call-done.w2_ref
  301.9 65.3 %mlp.1 = (f32[768,1152]{1,0:T(8,128)}, f32[768,1152]{1,0:T(8,128)}, bf16[4608,1152]{1,0:T(8,128)(2,1)}, bf16[4608,1152]{1,0:T(8,128)(2,1)}, f32[9,1,512]{2,1,0:T(1,128)}) custom-call(bf16[768,1152]{1,0:T(8,128)(2,1)} %fusion.11.x_ref, bf16[768,1152]{1,0:T(8,128)(2,1)} %get-tuple-element.40.g_ref, bf16[4608,1152]{1,0:T(8,128)(2,1)} %all-gather.6.cloned.1.call-done.w1_ref, ...), custom_call_target="tpu_custom_call" | custom-call | flops 48922361856 | bytes 53084160 | tf_op jit(solution)/shard_map/mlp/pallas_call | solution.py:231
  372.3 7.2 convert_reduce_fusion.1
  411.6 56.9 %psum.15 = f32[2,1152]{1,0:T(2,128)S(1)} all-reduce(f32[2,1152]{1,0:T(2,128)S(1)} %pad_maximum_fusion.6), channel_id=1, replica_groups=mesh['outer'=2,'core'=2,'part'=2,'group'=4] {'outer','core','part','group'}, use_global_device_ids=true, to_apply=%region_20.21 | all-reduce | flops 2304 | bytes 18432 | tf_op jit(solution)/shard_map/psum | solution.py:516
  473.3 59.6 %attend_back.1 = bf16[3072,864]{1,0:T(8,128)(2,1)} custom-call(s32[3]{0:T(128)} %compare_convert_fusion.single_ref, bf16[3072,864]{1,0:T(8,128)(2,1)} %add_convert_fusion.qkv_ref, bf16[3072,288]{1,0:T(8,128)(2,1)} %bitcast.175), custom_call_target="tpu_custom_call" | custom-call | flops 16106127360 | bytes 12386304 | tf_op jit(solution)/shard_map/attend_back/pallas_call | solution.py:178
  536.7 10.7 %convolution_convert_fusion.2 = bf16[864,1152]{1,0:T(8,128)(2,1)S(1)} fusion(bf16[3072,864]{1,0:T(8,128)(2,1)} %attend_back.1, bf16[3072,1152]{1,0:T(8,128)(2,1)} %copy-done.16), kind=kOutput, calls=%fused_computation.44 | convolution fusion | flops 6116290560 | bytes 14376960 | tf_op jit(solution)/shard_map/dot_general | solution.py:446
  547.9 13.8 %collective-permute-start.9 = (bf16[448,1152]{1,0:T(8,128)(2,1)S(1)}, bf16[448,1152]{1,0:T(8,128)(2,1)S(1)}, u32[]{:S(2)}, u32[]{:S(2)}) collective-permute-start(bf16[448,1152]{1,0:T(8,128)(2,1)S(1)} %select_bitcast_fusion), channel_id=1, source_target_pairs={{0,4},{4,0},{1,5},{5,1},{2,6},{6,2},{3,7},{7,3},{8,12},{12,8},{9,1... | collective-permute-start | bytes 3096584 | tf_op jit(solution)/shard_map/ppermute | solution.py:257
  561.7 8.8 convolution_convert_fusion
  577.7 50.8 %collective-permute-done.9 = bf16[448,1152]{1,0:T(8,128)(2,1)S(1)} collective-permute-done((bf16[448,1152]{1,0:T(8,128)(2,1)S(1)}, bf16[448,1152]{1,0:T(8,128)(2,1)S(1)}, u32[]{:S(2)}, u32[]{:S(2)}) %collective-permute-start.9) | collective-permute-done | bytes 1032224 | tf_op jit(solution)/shard_map/ppermute | solution.py:257
  644.5 9.3 %collective-permute-done.11 = bf16[224,1152]{1,0:T(8,128)(2,1)} collective-permute-done((bf16[224,1152]{1,0:T(8,128)(2,1)}, bf16[224,1152]{1,0:T(8,128)(2,1)}, u32[]{:S(2)}, u32[]{:S(2)}) %collective-permute-start.11) | collective-permute-done | bytes 516128 | tf_op jit(solution)/shard_map/ppermute | solution.py:257
  655.2 60.1 %collective-permute-done.7 = bf16[2,384,1152]{2,1,0:T(8,128)(2,1)} collective-permute-done((bf16[2,384,1152]{2,1,0:T(8,128)(2,1)}, bf16[2,384,1152]{2,1,0:T(8,128)(2,1)}, u32[]{:S(2)}, u32[]{:S(2)}) %collective-permute-start.7) | collective-permute-done | bytes 1769504 | tf_op jit(solution)/shard_map/ppermute | solution.py:257
  715.3 21.5 %collective-permute-done.6 = bf16[384,1152]{1,0:T(8,128)(2,1)} collective-permute-done((bf16[384,1152]{1,0:T(8,128)(2,1)}, bf16[384,1152]{1,0:T(8,128)(2,1)}, u32[]{:S(2)}, u32[]{:S(2)}) %collective-permute-start.6) | collective-permute-done | bytes 884768 | tf_op jit(solution)/shard_map/ppermute | solution.py:257
  743.5 22.9 %collective-permute-done.8 = bf16[384,1152]{1,0:T(8,128)(2,1)S(1)} collective-permute-done((bf16[384,1152]{1,0:T(8,128)(2,1)S(1)}, bf16[384,1152]{1,0:T(8,128)(2,1)S(1)}, u32[]{:S(2)}, u32[]{:S(2)}) %collective-permute-start.8) | collective-permute-done | bytes 884768 | tf_op jit(solution)/shard_map/ppermute | solution.py:257
  791.1 14.9 %all_gather.27 = f32[96,864]{1,0:T(8,128)S(1)} all-gather(f32[24,864]{1,0:T(8,128)S(1)} %fusion.26), channel_id=1, replica_groups=mesh['outer'=2,'core'=2,'part'=2,'group'=4] {'outer','core'}, dimensions={0}, use_global_device_ids=true | all-gather | bytes 414720 | tf_op jit(solution)/shard_map/all_gather | solution.py:505
  814.9 64.1 %all-reduce.6.cloned.1.call-done = f32[24,1152]{1,0:T(8,128)} async-done(((f32[24,1152]{1,0:T(8,128)}), f32[24,1152]{1,0:T(8,128)}) %all-reduce.6.cloned.1.call-update) | async-done | bytes 110608 | tf_op jit(solution)/shard_map/psum | solution.py:509
  (280 shorter events, 182.4 us)
Async XLA Ops:
  7.2 248.1 %all-gather.10.cloned.1.call-start = ((), (), s32[]{:S(2)}) async-start(), calls=%async_computation.13 | async-start | bytes 3133440 | tf_op jit(solution)/shard_map/all_gather | solution.py:362
  9.8 285.8 %all-gather.6.cloned.1.call-start = ((), (), s32[]{:S(2)}) async-start(), calls=%async_computation.7 | async-start | bytes 11280384 | tf_op jit(solution)/shard_map/all_gather | solution.py:366
  11.9 290.0 %all-gather.8.cloned.1.call-start = ((), (), s32[]{:S(2)}) async-start(), calls=%async_computation.8 | async-start | bytes 11280384 | tf_op jit(solution)/shard_map/all_gather | solution.py:367
  15.8 16.5 %all-to-all-start = ((f32[8,3,864]{2,1,0:T(4,128)}), f32[8,3,864]{2,1,0:T(4,128)S(1)}, u32[]{:S(2)}, u32[]{:S(2)}) async-start(f32[8,3,864]{2,1,0:T(4,128)} %reshape.377), calls=%async_computation | async-start | bytes 229376 | tf_op jit(solution)/shard_map/all_to_all | solution.py:387
  39.1 94.7 %collective-permute-start.1 = (bf16[768,1152]{1,0:T(8,128)(2,1)}, bf16[768,1152]{1,0:T(8,128)(2,1)}, u32[]{:S(2)}, u32[]{:S(2)}) collective-permute-start(bf16[768,1152]{1,0:T(8,128)(2,1)} %get-tuple-element.71), channel_id=1, source_target_pairs={{0,2},{1,3},{2,0},{3,1},{4,6},{5,7},{6,4},{7,5},{8,10},{9,11},{10,... | collective-permute-start | bytes 5308424 | tf_op jit(solution)/shard_map/ppermute | solution.py:257
  39.1 96.0 %collective-permute-start = (bf16[768,1152]{1,0:T(8,128)(2,1)}, bf16[768,1152]{1,0:T(8,128)(2,1)}, u32[]{:S(2)}, u32[]{:S(2)}) collective-permute-start(bf16[768,1152]{1,0:T(8,128)(2,1)} %get-tuple-element.71), channel_id=1, source_target_pairs={{0,1},{1,0},{2,3},{3,2},{4,5},{5,4},{6,7},{7,6},{8,9},{9,8},{10,11... | collective-permute-start | bytes 5308424 | tf_op jit(solution)/shard_map/ppermute | solution.py:257
  40.7 95.8 %collective-permute-start.4 = (bf16[432,1152]{1,0:T(8,128)(2,1)S(1)}, bf16[432,1152]{1,0:T(8,128)(2,1)}, u32[]{:S(2)}, u32[]{:S(2)}) collective-permute-start(bf16[432,1152]{1,0:T(8,128)(2,1)S(1)} %bitcast.179), channel_id=1, source_target_pairs={{0,4},{4,0},{1,5},{5,1},{2,6},{6,2},{3,7},{7,3},{8,12},{12,8},{9,1... | collective-permute-start | bytes 2985992 | tf_op jit(solution)/shard_map/ppermute | solution.py:257
  135.1 28.7 %collective-permute-start.2 = (bf16[384,1152]{1,0:T(8,128)(2,1)S(1)}, bf16[384,1152]{1,0:T(8,128)(2,1)S(1)}, u32[]{:S(2)}, u32[]{:S(2)}) collective-permute-start(bf16[384,1152]{1,0:T(8,128)(2,1)S(1)} %slice.116), channel_id=1, source_target_pairs={{0,1},{1,0},{2,3},{3,2},{4,5},{5,4},{6,7},{7,6},{8,9},{9,8},{10,11... | collective-permute-start | bytes 2654216 | tf_op jit(solution)/shard_map/ppermute | solution.py:257
  136.4 53.9 %collective-permute-start.3 = (bf16[384,1152]{1,0:T(8,128)(2,1)S(1)}, bf16[384,1152]{1,0:T(8,128)(2,1)S(1)}, u32[]{:S(2)}, u32[]{:S(2)}) collective-permute-start(bf16[384,1152]{1,0:T(8,128)(2,1)S(1)} %slice.117), channel_id=1, source_target_pairs={{0,2},{1,3},{2,0},{3,1},{4,6},{5,7},{6,4},{7,5},{8,10},{9,11},{10,... | collective-permute-start | bytes 2654216 | tf_op jit(solution)/shard_map/ppermute | solution.py:257
  247.4 35.0 %all-to-all-start.1 = ((bf16[4,768,288]{1,2,0:T(8,128)(2,1)}), bf16[4,768,288]{1,2,0:T(8,128)(2,1)}, u32[]{:S(2)}, u32[]{:S(2)}) async-start(bf16[4,768,288]{1,2,0:T(8,128)(2,1)} %copy.51), calls=%async_computation.1 | async-start | bytes 3538944 | tf_op jit(solution)/shard_map/all_to_all | solution.py:408
  251.8 379.2 %reduce-scatter.4.cloned.1.call-start = ((), (), s32[]{:S(2)}) async-start(), calls=%async_computation.10 | async-start | bytes 3133440 | tf_op jit(solution)/shard_map/reduce_scatter | solution.py:441
  387.2 402.5 %reduce-scatter.8.cloned.1.call-start = ((), (), s32[]{:S(2)}) async-start(), calls=%async_computation.12 | async-start | bytes 11280384 | tf_op jit(solution)/shard_map/reduce_scatter | solution.py:424
  400.8 68.3 %all-to-all-start.2 = ((bf16[4,768,288]{1,2,0:T(8,128)(2,1)}), bf16[4,768,288]{1,2,0:T(8,128)(2,1)}, u32[]{:S(2)}, u32[]{:S(2)}) async-start(bf16[4,768,288]{1,2,0:T(8,128)(2,1)} %bitcast.168), calls=%async_computation.2 | async-start | bytes 3538944 | tf_op jit(solution)/shard_map/all_to_all | solution.py:434
  405.2 406.7 %reduce-scatter.6.cloned.1.call-start = ((), (), s32[]{:S(2)}) async-start(), calls=%async_computation.11 | async-start | bytes 11280384 | tf_op jit(solution)/shard_map/reduce_scatter | solution.py:425
  547.9 80.6 %collective-permute-start.9 = (bf16[448,1152]{1,0:T(8,128)(2,1)S(1)}, bf16[448,1152]{1,0:T(8,128)(2,1)S(1)}, u32[]{:S(2)}, u32[]{:S(2)}) collective-permute-start(bf16[448,1152]{1,0:T(8,128)(2,1)S(1)} %select_bitcast_fusion), channel_id=1, source_target_pairs={{0,4},{4,0},{1,5},{5,1},{2,6},{6,2},{3,7},{7,3},{8,12},{12,8},{9,1... | collective-permute-start | bytes 3096584 | tf_op jit(solution)/shard_map/ppermute | solution.py:257
  575.1 64.9 %collective-permute-start.5 = (bf16[2,384,1152]{2,1,0:T(8,128)(2,1)}, bf16[2,384,1152]{2,1,0:T(8,128)(2,1)}, u32[]{:S(2)}, u32[]{:S(2)}) collective-permute-start(bf16[2,384,1152]{2,1,0:T(8,128)(2,1)} %pad_maximum_fusion.2), channel_id=1, source_target_pairs={{0,1},{1,0},{2,3},{3,2},{4,5},{5,4},{6,7},{7,6},{8,9},{9,8},{10,11... | collective-permute-start | bytes 5308424 | tf_op jit(solution)/shard_map/ppermute | solution.py:257
  633.9 81.4 %collective-permute-start.7 = (bf16[2,384,1152]{2,1,0:T(8,128)(2,1)}, bf16[2,384,1152]{2,1,0:T(8,128)(2,1)}, u32[]{:S(2)}, u32[]{:S(2)}) collective-permute-start(bf16[2,384,1152]{2,1,0:T(8,128)(2,1)} %pad_maximum_fusion.3), channel_id=1, source_target_pairs={{0,2},{1,3},{2,0},{3,1},{4,6},{5,7},{6,4},{7,5},{8,10},{9,11},{10,... | collective-permute-start | bytes 5308424 | tf_op jit(solution)/shard_map/ppermute | solution.py:257
  642.7 94.0 %collective-permute-start.6 = (bf16[384,1152]{1,0:T(8,128)(2,1)}, bf16[384,1152]{1,0:T(8,128)(2,1)}, u32[]{:S(2)}, u32[]{:S(2)}) collective-permute-start(bf16[384,1152]{1,0:T(8,128)(2,1)} %fusion.18), channel_id=1, source_target_pairs={{0,2},{1,3},{2,0},{3,1},{4,6},{5,7},{6,4},{7,5},{8,10},{9,11},{10,... | collective-permute-start | bytes 2654216 | tf_op jit(solution)/shard_map/ppermute | solution.py:257
  655.1 86.0 %collective-permute-start.12 = (bf16[224,1152]{1,0:T(8,128)(2,1)S(1)}, bf16[224,1152]{1,0:T(8,128)(2,1)S(1)}, u32[]{:S(2)}, u32[]{:S(2)}) collective-permute-start(bf16[224,1152]{1,0:T(8,128)(2,1)S(1)} %add_convert_fusion.4), channel_id=1, source_target_pairs={{0,8},{8,0},{1,9},{9,1},{2,10},{10,2},{3,11},{11,3},{4,12},{12,4},... | collective-permute-start | bytes 1548296 | tf_op jit(solution)/shard_map/ppermute | solution.py:257
  739.5 26.9 %collective-permute-start.8 = (bf16[384,1152]{1,0:T(8,128)(2,1)S(1)}, bf16[384,1152]{1,0:T(8,128)(2,1)S(1)}, u32[]{:S(2)}, u32[]{:S(2)}) collective-permute-start(bf16[384,1152]{1,0:T(8,128)(2,1)S(1)} %get-tuple-element.44), channel_id=1, source_target_pairs={{0,1},{1,0},{2,3},{3,2},{4,5},{5,4},{6,7},{7,6},{8,9},{9,8},{10,11... | collective-permute-start | bytes 2654216 | tf_op jit(solution)/shard_map/ppermute | solution.py:257
  782.1 96.9 %all-reduce.6.cloned.1.call-start = ((), (), s32[]{:S(2)}) async-start(), calls=%async_computation.9 | async-start | bytes 221184 | tf_op jit(solution)/shard_map/psum | solution.py:509
  789.7 23.8 %collective-permute-start.17 = (bf16[288,1152]{1,0:T(8,128)(2,1)}, bf16[288,1152]{1,0:T(8,128)(2,1)}, u32[]{:S(2)}, u32[]{:S(2)}) collective-permute-start(bf16[288,1152]{1,0:T(8,128)(2,1)} %reduce-scatter.8.cloned.1.call-done), channel_id=1, source_target_pairs={{0,16},{16,0},{1,17},{17,1},{2,18},{18,2},{3,19},{19,3},{4,20},{20... | collective-permute-start | bytes 1990664 | tf_op jit(solution)/shard_map/ppermute | solution.py:257
  811.9 68.7 %collective-permute-start.15 = (bf16[288,1152]{1,0:T(8,128)(2,1)}, bf16[288,1152]{1,0:T(8,128)(2,1)}, u32[]{:S(2)}, u32[]{:S(2)}) collective-permute-start(bf16[288,1152]{1,0:T(8,128)(2,1)} %reduce-scatter.6.cloned.1.call-done), channel_id=1, source_target_pairs={{0,16},{16,0},{1,17},{17,1},{2,18},{18,2},{3,19},{19,3},{4,20},{20... | collective-permute-start | bytes 1990664 | tf_op jit(solution)/shard_map/ppermute | solution.py:257
  814.8 67.4 %collective-permute-start.18 = (bf16[288,1152]{1,0:T(8,128)(2,1)S(1)}, bf16[288,1152]{1,0:T(8,128)(2,1)S(1)}, u32[]{:S(2)}, u32[]{:S(2)}) collective-permute-start(bf16[288,1152]{1,0:T(8,128)(2,1)S(1)} %add_convert_fusion.2), channel_id=1, source_target_pairs={{0,8},{8,0},{1,9},{9,1},{2,10},{10,2},{3,11},{11,3},{4,12},{12,4},... | collective-permute-start | bytes 1990664 | tf_op jit(solution)/shard_map/ppermute | solution.py:257
  (51 other events, 594.3 us)
Sparse Core Ops, SparseCore 0:
  10.8 73.1 all-gather.9
  86.8 109.5 all-gather.5
  199.2 102.6 all-gather.7
  387.3 73.9 reduce-scatter.3
  465.3 153.1 reduce-scatter.7
  622.4 159.1 reduce-scatter.5
  808.3 70.6 all-reduce.5

commit v2 on v1

--- a/solution.py
+++ b/solution.py
@@ -303,16 +303,49 @@
     )
 
 
+def powers(size):
+    return [1 << b for b in range(size.bit_length() - 1)] if size & (size - 1) == 0 else None
+
+
+def sum_axis(value, axis, size):
+    masks = powers(size)
+    if masks is None:
+        return lax.psum(value, axis)
+    for mask in masks:
+        value = value + swap(value, axis, size, mask)
+    return value
+
+
+def gather_axis(value, axis, size):
+    masks = powers(size)
+    if masks is None:
+        return lax.all_gather(value, axis, axis=0, tiled=True)
+    me = lax.axis_index(axis)
+    for mask in masks:
+        other = swap(value, axis, size, mask)
+        first = jnp.bitwise_and(me, mask) == 0
+        value = jnp.concatenate(
+            [jnp.where(first, value, other), jnp.where(first, other, value)], axis=0
+        )
+    return value
+
+
 def sum_outer(value, size):
     total = value.astype(F32)
-    if size & (size - 1):
+    masks = powers(size)
+    if masks is None:
         return lax.psum(value, OUTER).astype(F32)
-    mask = 1
-    while mask < size:
-        total = total + swap(total.astype(BF16), OUTER, size, mask).astype(F32)
-        total = total if mask * 2 >= size else total.astype(BF16).astype(F32)
-        mask *= 2
+    for mask in masks:
+        low = total.astype(BF16)
+        total = low.astype(F32) + swap(low, OUTER, size, mask).astype(F32)
     return total
+
+
+def sum_cores(value):
+    half = value.shape[0] // 2
+    sent = lax.dynamic_slice_in_dim(value, (1 - lax.axis_index(CORE)) * half, half)
+    got = swap(sent.astype(BF16), CORE, 2, 1)
+    return core_half(value).astype(F32) + got.astype(F32)
 
 
 def join_cores(own):
@@ -322,9 +355,19 @@
     return jnp.concatenate([jnp.where(first, own, other), jnp.where(first, other, own)])
 
 
+def scatter_weight(value):
+    value = sum_cores(value).astype(BF16)
+    return lax.psum_scatter(value, HEAD, scatter_dimension=0, tiled=True)
+
+
 def core_half(value):
     half = value.shape[0] // 2
     return lax.dynamic_slice_in_dim(value, lax.axis_index(CORE) * half, half)
+
+
+def spread_row(row, copies, width):
+    row = jnp.pad(row, (0, width - row.shape[0]))
+    return jnp.broadcast_to(row, (copies, 1, width))
 
 
 def local(
@@ -356,13 +399,8 @@
     heads = part_size * cols // HEAD_DIM
     head_at = lax.axis_index(HEAD)
 
-    proj_half, fc1_half = cols // 2, ff_here // 2
-    bias_row = jnp.pad(core_half(b_fc1)[None, :], ((0, 0), (0, width - fc1_half)))
-    proj_sent = jnp.concatenate([core_half(w_proj), bias_row])
-    proj_rows = lax.all_gather(proj_sent, SPREAD, axis=0)
-    proj_rows = proj_rows.reshape(2 * head_size, proj_half + 1, width)
-    proj_full = proj_rows[:, :proj_half].reshape(-1, width)
-    bias_fc1 = proj_rows[:, proj_half, :fc1_half].reshape(-1).astype(F32)
+    proj_half = cols // 2
+    proj_full = lax.all_gather(core_half(w_proj), SPREAD, axis=0, tiled=True)
     fc1_full = lax.all_gather(core_half(w_fc1.T), SPREAD, axis=0, tiled=True)
     fc2_full = lax.all_gather(core_half(w_fc2), SPREAD, axis=0, tiled=True)
     qkv_own = jnp.transpose(w_qkv, (1, 2, 0)).reshape(3 * cols, width)
@@ -374,18 +412,31 @@
         )
     else:
         qkv_weight = lax.all_gather(qkv_own, PART, axis=0, tiled=True)
-    bias_own = jnp.concatenate([bias_qv[0], jnp.zeros((cols,), bias_qv.dtype), bias_qv[1]])
-    qkv_bias = lax.all_gather(bias_own, PART, axis=0, tiled=True).astype(F32)
-
     unit_ids = segment_ids[::unit] - lax.axis_index(DP) * slots
     pick = (unit_ids[:, None] == jnp.arange(slots, dtype=jnp.int32)[None, :]).astype(F32)
     cond_act, silu_back = jax.vjp(jax.nn.silu, cond)
     cond_low = cond_act.astype(BF16)
-    cond_all = lax.all_gather(cond_low, DP, axis=0, tiled=True)
+    cond_all = gather_axis(gather_axis(cond_low, CORE, 2), OUTER, outer_size)
     mod_part = jnp.dot(cond_low, w_ada, preferred_element_type=F32) + b_ada.astype(F32)
     mod_sent = jnp.dot(pick, mod_part, precision=TOP).reshape(head_size, units, ada_cols)
+    bias_own = jnp.concatenate([bias_qv[0], jnp.zeros((cols,), bias_qv.dtype), bias_qv[1]])
+    mod_sent = jnp.concatenate(
+        [
+            mod_sent,
+            spread_row(b_fc1.astype(F32), head_size, ada_cols),
+            spread_row(bias_own.astype(F32), head_size, ada_cols),
+        ],
+        axis=1,
+    )
     mod_got = lax.all_to_all(mod_sent, HEAD, split_axis=0, concat_axis=0, tiled=True)
-    modulation = jnp.transpose(mod_got, (1, 0, 2)).reshape(units, 6, 1, width)
+    bias_fc1 = jnp.transpose(
+        mod_got[:, units, :ff_here].reshape(head_size, 2, ff_here // 2), (1, 0, 2)
+    ).reshape(-1)
+    bias_parts = mod_got[:, units + 1, : 3 * cols].reshape(part_size, group_size, 3 * cols)
+    qkv_bias = lax.dynamic_slice_in_dim(
+        bias_parts, lax.axis_index(GROUP), 1, axis=1
+    ).reshape(part_size * 3 * cols)
+    modulation = jnp.transpose(mod_got[:, :units], (1, 0, 2)).reshape(units, 6, 1, width)
     shift_a, scale_a, gate_a, shift_m, scale_m, gate_m = [modulation[:, i] for i in range(6)]
 
     def by_unit(value):
@@ -421,24 +472,32 @@
     branch_m, grad_mlp_in, grad_fc1, grad_fc2, grad_b1 = mlp(
         mlp_in, grad_branch_m, fc1_full, fc2_full, bias_fc1
     )
-    grad_fc2 = lax.psum_scatter(grad_fc2, SPREAD, scatter_dimension=0, tiled=True)
-    grad_fc1 = lax.psum_scatter(grad_fc1, SPREAD, scatter_dimension=0, tiled=True)
+    grad_fc2 = scatter_weight(grad_fc2)
+    grad_fc1 = scatter_weight(grad_fc1)
     branch_m = by_unit(branch_m) + b_fc2.astype(F32)
     grad_mlp_in = by_unit(grad_mlp_in)
     output = flat((mid + gate_m * branch_m).astype(BF16))
     grad_mid = cotan + norm_back(grad_mlp_in * (1.0 + scale_m), normed_m, inverse_m)
     grad_branch_a = flat((gate_a * grad_mid).astype(BF16))
+    bias_sums = jnp.concatenate(
+        [
+            jnp.sum(grad_branch_a.astype(F32), axis=0),
+            jnp.sum(grad_branch_m.astype(F32), axis=0),
+            grad_b1.reshape(-1),
+        ]
+    ).reshape(-1, width)
+    for axis, size in ((CORE, 2), (OUTER, outer_size), (GROUP, group_size), (PART, part_size)):
+        bias_sums = sum_axis(bias_sums, axis, size)
+    grad_b_proj, grad_b_fc2 = bias_sums[0], bias_sums[1]
+    grad_b1 = lax.dynamic_slice_in_dim(
+        bias_sums[2:].reshape(2, head_size, ff_here // 2), head_at, 1, axis=1
+    ).reshape(-1)
     grad_mix = lax.dot_general(grad_branch_a, proj_full, NT, preferred_element_type=F32)
     grad_mix = grad_mix.astype(BF16).reshape(rows, 2, part_size, group_size, proj_half)
     grad_mix = jnp.transpose(grad_mix, (3, 0, 2, 1, 4)).reshape(group_size, rows, -1)
     grad_mix = lax.all_to_all(grad_mix, GROUP, split_axis=0, concat_axis=0)
     grad_proj = lax.dot_general(mix, grad_branch_a, TN, preferred_element_type=F32).astype(BF16)
-    b1_row = jnp.pad(
-        grad_b1.reshape(2 * head_size, 1, fc1_half).astype(BF16),
-        ((0, 0), (0, 0), (0, width - fc1_half)),
-    )
-    grad_proj = jnp.concatenate([grad_proj.reshape(2 * head_size, proj_half, width), b1_row], axis=1)
-    grad_proj = lax.psum_scatter(grad_proj, SPREAD, scatter_dimension=0, tiled=True)[0]
+    grad_proj = scatter_weight(grad_proj)
     grad_qkv = attend_back(single, qkv, grad_mix.reshape(-1, heads * HEAD_DIM), heads, cols)
     attn_grad_part = jnp.dot(grad_qkv, qkv_weight, preferred_element_type=F32).astype(BF16)
     grad_attn_in = by_unit(scatter_group(attn_grad_part, group_size))
@@ -460,14 +519,7 @@
         grad_w_qkv = lax.psum_scatter(
             grad_w_qkv, PART, scatter_dimension=0, tiled=True
         )[0].astype(F32)
-    half = grad_w_qkv.shape[0] // 2
-    other = swap(
-        lax.dynamic_slice_in_dim(grad_w_qkv, (1 - lax.axis_index(CORE)) * half, half).astype(BF16),
-        CORE,
-        2,
-        1,
-    )
-    grad_w_qkv = (core_half(grad_w_qkv) + other.astype(F32)).astype(BF16)
+    grad_w_qkv = sum_cores(grad_w_qkv).astype(BF16)
     grad_w_qkv = join_cores(sum_outer(grad_w_qkv, outer_size)).astype(F32)
     grad_bias = grad_w_qkv[3 * cols, : 3 * cols]
     grad_bias_qv = jnp.stack([grad_bias[:cols], grad_bias[2 * cols :]])
@@ -476,9 +528,6 @@
     grad_fc2 = join_cores(sum_outer(grad_fc2, outer_size)).astype(F32)
     grad_fc1 = join_cores(sum_outer(grad_fc1, outer_size)).astype(F32).T
     grad_proj = join_cores(sum_outer(grad_proj, outer_size)).astype(F32)
-    grad_proj = grad_proj.reshape(2, proj_half + 1, width)
-    grad_b1 = grad_proj[:, proj_half, :fc1_half].reshape(-1)
-    grad_proj = grad_proj[:, :proj_half].reshape(cols, width)
 
     grad_tokens = flat(
         (grad_mid + norm_back(grad_attn_in * (1.0 + scale_a), normed_a, inverse_a)).astype(BF16)
@@ -502,18 +551,12 @@
     grad_mod = lax.dot_general(
         pick, unit_grad.reshape(head_size * units, ada_cols), TN, precision=TOP
     )
-    grad_mod_all = lax.all_gather(grad_mod, DP, axis=0, tiled=True)
+    grad_mod_all = gather_axis(gather_axis(grad_mod, CORE, 2), OUTER, outer_size)
     grad_w_ada = lax.dot_general(cond_all.astype(F32), grad_mod_all, TN, precision=TOP)
     grad_b_ada = jnp.sum(grad_mod_all, axis=0)
     grad_cond_part = lax.dot_general(grad_mod, w_ada.astype(F32), NT, precision=TOP)
-    grad_cond = silu_back(lax.psum(grad_cond_part, HEAD))[0]
-    bias_parts = jnp.stack(
-        [
-            jnp.sum(grad_branch_a.astype(F32), axis=0),
-            jnp.sum(grad_branch_m.astype(F32), axis=0),
-        ]
-    )
-    bias_sums = lax.psum(bias_parts, EVERY)
+    grad_cond_sum = sum_axis(sum_axis(grad_cond_part, GROUP, group_size), PART, part_size)
+    grad_cond = silu_back(grad_cond_sum)[0]
     return (
         output,
         grad_tokens,
@@ -523,11 +566,11 @@
         grad_w_qkv,
         grad_bias_qv,
         grad_proj,
-        bias_sums[0],
+        grad_b_proj,
         grad_fc1,
         grad_b1,
         grad_fc2,
-        bias_sums[1],
+        grad_b_fc2,
     )
 
 

time: 904 us -> 835 us (0.924)
  blocking collectives: 158 us -> 0 us
  waiting for transfers between devices: 325 us -> 386 us
  other arithmetic: 70.2 us -> 86.9 us
    ppermute x19 -> x34, waiting for transfers between devices: 226 us -> 328 us  [swap(): return lax.ppermute(value, axis, xor_pairs(size, mask))]
    unnamed x1 -> x0, blocking collectives: 80.1 us -> none
    psum x1 -> x0, waiting for transfers between devices: 64.1 us -> none  [local(): grad_cond = silu_back(lax.psum(grad_cond_part, HEAD))[0]]
    psum x1 -> x0, blocking collectives: 56.9 us -> none  [local(): bias_sums = lax.psum(bias_parts, EVERY)]
    all_gather x2 -> x0, blocking collectives: 21 us -> none  [the longest x1 14.9 us: local(): grad_mod_all = lax.all_gather(grad_mod, DP, axis=0, tiled=True)]
    convert_element_type x4, other arithmetic: 1.92 us -> 18.6 us  [the longest x3 17.4 us: scatter_weight(): value = sum_cores(value).astype(BF16)]
    all_to_all x1, waiting for transfers between devices: 21.9 us -> 37.6 us  [local(): lax.all_to_all(mix_part.reshape(group_size, rows, heads * HEAD_DIM), GROU...]
    dynamic_slice x0 -> x5, local copies, waits for them, and re-layouts: none -> 10.6 us  [the longest x3 10.6 us: sum_cores(): lax.dynamic_slice_in_dim(value, (1 - lax.axis_index(CORE)) * half, half)]
  transfers between devices with their start and end apart: 30 -> 44, of which waited for: 16 -> 22; matrix products, arithmetic and copies ran while one was open for 16% -> 22% of each run, Pallas kernels for 11% -> 12%
where the time goes in v2:
time: 835 us; the launch traced here: 821 us
  waiting for transfers between devices  386 us (46%)
  Pallas kernels  165 us (20%)
  other arithmetic  86.9 us (10%)
  local copies, waits for them, and re-layouts  69.6 us (8%)
  matrix products  51.1 us (6%)
  starting transfers between devices  46.1 us (6%)
  between operations  15.7 us (2%)
    ppermute x34, waiting for transfers between devices, swap(): return lax.ppermute(value, axis, xor_pairs(size, mask))  328 us
    pallas_call x1, Pallas kernels, mlp(): pl.pallas_call(mlp_kernel, grid=(tiles,), in_specs=[whole, whole, piece,...  65.3 us
    pallas_call x1, Pallas kernels, attend_back(): pl.pallas_call(functools.partial(attend_back_kernel, heads, cols), grid_s...  59.3 us
    pallas_call x1, Pallas kernels, attend(): pl.pallas_call(functools.partial(attend_kernel, heads, cols), grid_spec=p...  40.2 us
    all_to_all x1, waiting for transfers between devices, local(): lax.all_to_all(mix_part.reshape(group_size, rows, heads * HEAD_DIM), GROU...  37.6 us
    ppermute x34, starting transfers between devices, swap(): return lax.ppermute(value, axis, xor_pairs(size, mask))  24.5 us
    unnamed x116, local copies, waits for them, and re-layouts  18.4 us
    convert_element_type x3, other arithmetic, scatter_weight(): value = sum_cores(value).astype(BF16)  17.4 us
  transfers between devices with their start and end apart: 44, of which 22 were waited for; matrix products, arithmetic and copies ran while one was open for 22% of the time, Pallas kernels for 12%

profile of v2, /device:TPU:0, one launch (start us, length us, event | category | flops | bytes accessed | tf_op | source)
XLA Modules:
  0.0 820.7 jit_solution(8391971416353104892)
XLA Ops:
  15.4 7.3 all-to-all-start
  26.6 8.4 %all-to-all-done = f32[8,5,864]{2,1,0:T(8,128)S(1)} async-done(((f32[8,5,864]{2,1,0:T(8,128)}), f32[8,5,864]{2,1,0:T(8,128)S(1)}, u32[]{:S(2)}, u32[]{:S(2)}) %all-to-all-start) | async-done | bytes 138272 | tf_op jit(solution)/shard_map/all_to_all | solution.py:431
  47.9 84.6 %collective-permute-done.1 = bf16[768,1152]{1,0:T(8,128)(2,1)} collective-permute-done((bf16[768,1152]{1,0:T(8,128)(2,1)}, bf16[768,1152]{1,0:T(8,128)(2,1)}, u32[]{:S(2)}, u32[]{:S(2)}) %collective-permute-start.1) | collective-permute-done | bytes 1769504 | tf_op jit(solution)/shard_map/ppermute | solution.py:257
  142.1 26.1 %collective-permute-done.2 = bf16[384,1152]{1,0:T(8,128)(2,1)S(1)} collective-permute-done((bf16[384,1152]{1,0:T(8,128)(2,1)S(1)}, bf16[384,1152]{1,0:T(8,128)(2,1)S(1)}, u32[]{:S(2)}, u32[]{:S(2)}) %collective-permute-start.2) | collective-permute-done | bytes 884768 | tf_op jit(solution)/shard_map/ppermute | solution.py:257
  168.3 21.0 %collective-permute-done.3 = bf16[384,1152]{1,0:T(8,128)(2,1)S(1)} collective-permute-done((bf16[384,1152]{1,0:T(8,128)(2,1)S(1)}, bf16[384,1152]{1,0:T(8,128)(2,1)S(1)}, u32[]{:S(2)}, u32[]{:S(2)}) %collective-permute-start.3) | collective-permute-done | bytes 884768 | tf_op jit(solution)/shard_map/ppermute | solution.py:257
  192.3 9.7 %add_convert_fusion.qkv_ref = bf16[3072,864]{1,0:T(8,128)(2,1)} fusion(f32[864]{0:T(1024)S(1)} %add.385, bf16[3072,1152]{1,0:T(8,128)(2,1)S(1)} %constant_dynamic-update-slice_fusion.6, bf16[432,1152]{1,0:T(8,128)(2,1)S(1)} %get-tuple-element.57, bf16[432,1152]{1,0:T(8,128)(2,1)S(1)} %get-tuple-element.56), kind=kOutput, calls=%fused_computation.3 | convolution fusion | flops 6124584960 | bytes 14380416 | tf_op jit(solution)/shard_map/dot_general | solution.py:452
  201.9 40.2 %attend.1 = bf16[3072,288]{1,0:T(8,128)(2,1)} custom-call(s32[3]{0:T(128)} %compare_convert_fusion.single_ref, bf16[3072,864]{1,0:T(8,128)(2,1)} %add_convert_fusion.qkv_ref), custom_call_target="tpu_custom_call" | custom-call | flops 6442450944 | bytes 7077888 | tf_op jit(solution)/shard_map/attend/pallas_call | solution.py:91
  255.9 37.6 %all-to-all-done.1 = bf16[4,768,288]{1,2,0:T(8,128)(2,1)} async-done(((bf16[4,768,288]{1,2,0:T(8,128)(2,1)}), bf16[4,768,288]{1,2,0:T(8,128)(2,1)}, u32[]{:S(2)}, u32[]{:S(2)}) %all-to-all-start.1) | async-done | bytes 1769504 | tf_op jit(solution)/shard_map/all_to_all | solution.py:459
  296.3 7.8 fusion.49
  313.1 65.3 %mlp.1 = (f32[768,1152]{1,0:T(8,128)}, f32[768,1152]{1,0:T(8,128)}, bf16[4608,1152]{1,0:T(8,128)(2,1)}, bf16[4608,1152]{1,0:T(8,128)(2,1)}, f32[9,1,512]{2,1,0:T(1,128)}) custom-call(bf16[768,1152]{1,0:T(8,128)(2,1)} %fusion.10.x_ref, bf16[768,1152]{1,0:T(8,128)(2,1)} %get-tuple-element.40.g_ref, bf16[4608,1152]{1,0:T(8,128)(2,1)} %all-gather.6.cloned.1.call-done.w1_ref, ...), custom_call_target="tpu_custom_call" | custom-call | flops 48922361856 | bytes 53084160 | tf_op jit(solution)/shard_map/mlp/pallas_call | solution.py:231
  389.0 8.2 convert_reduce_fusion.1
  425.3 8.0 add_convert_fusion.1
  442.2 9.3 %collective-permute-done.25 = f32[6,1152]{1,0:T(8,128)S(1)} collective-permute-done((f32[6,1152]{1,0:T(8,128)S(1)}, f32[6,1152]{1,0:T(8,128)S(1)}, u32[]{:S(2)}, u32[]{:S(2)}) %collective-permute-start.25) | collective-permute-done | bytes 27680 | tf_op jit(solution)/shard_map/ppermute | solution.py:257
  467.7 59.3 %attend_back.1 = bf16[3072,864]{1,0:T(8,128)(2,1)} custom-call(s32[3]{0:T(128)} %compare_convert_fusion.single_ref, bf16[3072,864]{1,0:T(8,128)(2,1)} %add_convert_fusion.qkv_ref, bf16[3072,288]{1,0:T(8,128)(2,1)} %bitcast.165), custom_call_target="tpu_custom_call" | custom-call | flops 16106127360 | bytes 12386304 | tf_op jit(solution)/shard_map/attend_back/pallas_call | solution.py:178
  530.5 10.4 %convolution_convert_fusion.2 = bf16[864,1152]{1,0:T(8,128)(2,1)S(1)} fusion(bf16[3072,864]{1,0:T(8,128)(2,1)} %attend_back.1, bf16[3072,1152]{1,0:T(8,128)(2,1)} %copy-done.17), kind=kOutput, calls=%fused_computation.44 | convolution fusion | flops 6116290560 | bytes 14376960 | tf_op jit(solution)/shard_map/dot_general | solution.py:505
  545.5 8.7 %convolution_convert_fusion = bf16[3072,1152]{1,0:T(8,128)(2,1)S(1)} fusion(bf16[3072,864]{1,0:T(8,128)(2,1)S(1)} %copy-done.22, bf16[432,1152]{1,0:T(8,128)(2,1)S(1)} %copy-done.30, bf16[432,1152]{1,0:T(8,128)(2,1)S(1)} %copy-done.28), kind=kOutput, calls=%fused_computation.2 | convolution fusion | flops 6122815488 | bytes 14376960 | tf_op jit(solution)/shard_map/dot_general | solution.py:502
  558.0 6.4 add_convert_fusion.2
  567.4 46.4 %collective-permute-done.16 = bf16[448,1152]{1,0:T(8,128)(2,1)} collective-permute-done((bf16[448,1152]{1,0:T(8,128)(2,1)}, bf16[448,1152]{1,0:T(8,128)(2,1)}, u32[]{:S(2)}, u32[]{:S(2)}) %collective-permute-start.16) | collective-permute-done | bytes 1032224 | tf_op jit(solution)/shard_map/ppermute | solution.py:257
  630.0 9.9 %collective-permute-done.18 = bf16[224,1152]{1,0:T(8,128)(2,1)S(1)} collective-permute-done((bf16[224,1152]{1,0:T(8,128)(2,1)S(1)}, bf16[224,1152]{1,0:T(8,128)(2,1)S(1)}, u32[]{:S(2)}, u32[]{:S(2)}) %collective-permute-start.18) | collective-permute-done | bytes 516128 | tf_op jit(solution)/shard_map/ppermute | solution.py:257
  640.2 56.2 %collective-permute-done.7 = bf16[2,384,1152]{2,1,0:T(8,128)(2,1)S(1)} collective-permute-done((bf16[2,384,1152]{2,1,0:T(8,128)(2,1)S(1)}, bf16[2,384,1152]{2,1,0:T(8,128)(2,1)S(1)}, u32[]{:S(2)}, u32[]{:S(2)}) %collective-permute-start.7) | collective-permute-done | bytes 1769504 | tf_op jit(solution)/shard_map/ppermute | solution.py:257
  696.4 18.9 %collective-permute-done.6 = bf16[384,1152]{1,0:T(8,128)(2,1)S(1)} collective-permute-done((bf16[384,1152]{1,0:T(8,128)(2,1)S(1)}, bf16[384,1152]{1,0:T(8,128)(2,1)S(1)}, u32[]{:S(2)}, u32[]{:S(2)}) %collective-permute-start.6) | collective-permute-done | bytes 884768 | tf_op jit(solution)/shard_map/ppermute | solution.py:257
  721.5 24.9 %collective-permute-done.8 = bf16[384,1152]{1,0:T(8,128)(2,1)S(1)} collective-permute-done((bf16[384,1152]{1,0:T(8,128)(2,1)S(1)}, bf16[384,1152]{1,0:T(8,128)(2,1)S(1)}, u32[]{:S(2)}, u32[]{:S(2)}) %collective-permute-start.8) | collective-permute-done | bytes 884768 | tf_op jit(solution)/shard_map/ppermute | solution.py:257
  762.8 7.2 all-to-all-done.3
  797.2 10.8 %collective-permute-done.29 = bf16[288,1152]{1,0:T(8,128)(2,1)S(1)} collective-permute-done((bf16[288,1152]{1,0:T(8,128)(2,1)}, bf16[288,1152]{1,0:T(8,128)(2,1)S(1)}, u32[]{:S(2)}, u32[]{:S(2)}) %collective-permute-start.29) | collective-permute-done | bytes 663584 | tf_op jit(solution)/shard_map/ppermute | solution.py:257
  (339 shorter events, 212.4 us)
Async XLA Ops:
  7.2 289.1 %all-gather.4.cloned.1.call-start = ((), (), s32[]{:S(2)}) async-start(), calls=%async_computation.7 | async-start | bytes 2820096 | tf_op jit(solution)/shard_map/all_gather | solution.py:403
  9.1 298.8 %all-gather.6.cloned.1.call-start = ((), (), s32[]{:S(2)}) async-start(), calls=%async_computation.8 | async-start | bytes 11280384 | tf_op jit(solution)/shard_map/all_gather | solution.py:404
  11.1 302.0 %all-gather.8.cloned.1.call-start = ((), (), s32[]{:S(2)}) async-start(), calls=%async_computation.9 | async-start | bytes 11280384 | tf_op jit(solution)/shard_map/all_gather | solution.py:405
  15.4 19.6 %all-to-all-start = ((f32[8,5,864]{2,1,0:T(8,128)}), f32[8,5,864]{2,1,0:T(8,128)S(1)}, u32[]{:S(2)}, u32[]{:S(2)}) async-start(f32[8,5,864]{2,1,0:T(8,128)} %pad_maximum_fusion.6), calls=%async_computation | async-start | bytes 458752 | tf_op jit(solution)/shard_map/all_to_all | solution.py:431
  42.4 90.1 %collective-permute-start.1 = (bf16[768,1152]{1,0:T(8,128)(2,1)}, bf16[768,1152]{1,0:T(8,128)(2,1)}, u32[]{:S(2)}, u32[]{:S(2)}) collective-permute-start(bf16[768,1152]{1,0:T(8,128)(2,1)} %get-tuple-element.83), channel_id=1, source_target_pairs={{0,2},{1,3},{2,0},{3,1},{4,6},{5,7},{6,4},{7,5},{8,10},{9,11},{10,... | collective-permute-start | bytes 5308424 | tf_op jit(solution)/shard_map/ppermute | solution.py:257
  43.2 91.5 %collective-permute-start = (bf16[768,1152]{1,0:T(8,128)(2,1)}, bf16[768,1152]{1,0:T(8,128)(2,1)}, u32[]{:S(2)}, u32[]{:S(2)}) collective-permute-start(bf16[768,1152]{1,0:T(8,128)(2,1)} %get-tuple-element.83), channel_id=1, source_target_pairs={{0,1},{1,0},{2,3},{3,2},{4,5},{5,4},{6,7},{7,6},{8,9},{9,8},{10,11... | collective-permute-start | bytes 5308424 | tf_op jit(solution)/shard_map/ppermute | solution.py:257
  44.1 91.9 %collective-permute-start.4 = (bf16[432,1152]{1,0:T(8,128)(2,1)S(1)}, bf16[432,1152]{1,0:T(8,128)(2,1)}, u32[]{:S(2)}, u32[]{:S(2)}) collective-permute-start(bf16[432,1152]{1,0:T(8,128)(2,1)S(1)} %bitcast.169), channel_id=1, source_target_pairs={{0,4},{4,0},{1,5},{5,1},{2,6},{6,2},{3,7},{7,3},{8,12},{12,8},{9,1... | collective-permute-start | bytes 2985992 | tf_op jit(solution)/shard_map/ppermute | solution.py:257
  133.7 34.5 %collective-permute-start.2 = (bf16[384,1152]{1,0:T(8,128)(2,1)S(1)}, bf16[384,1152]{1,0:T(8,128)(2,1)S(1)}, u32[]{:S(2)}, u32[]{:S(2)}) collective-permute-start(bf16[384,1152]{1,0:T(8,128)(2,1)S(1)} %slice.117), channel_id=1, source_target_pairs={{0,1},{1,0},{2,3},{3,2},{4,5},{5,4},{6,7},{7,6},{8,9},{9,8},{10,11... | collective-permute-start | bytes 2654216 | tf_op jit(solution)/shard_map/ppermute | solution.py:257
  135.9 53.4 %collective-permute-start.3 = (bf16[384,1152]{1,0:T(8,128)(2,1)S(1)}, bf16[384,1152]{1,0:T(8,128)(2,1)S(1)}, u32[]{:S(2)}, u32[]{:S(2)}) collective-permute-start(bf16[384,1152]{1,0:T(8,128)(2,1)S(1)} %slice.118), channel_id=1, source_target_pairs={{0,2},{1,3},{2,0},{3,1},{4,6},{5,7},{6,4},{7,5},{8,10},{9,11},{10,... | collective-permute-start | bytes 2654216 | tf_op jit(solution)/shard_map/ppermute | solution.py:257
  246.4 47.1 %all-to-all-start.1 = ((bf16[4,768,288]{1,2,0:T(8,128)(2,1)}), bf16[4,768,288]{1,2,0:T(8,128)(2,1)}, u32[]{:S(2)}, u32[]{:S(2)}) async-start(bf16[4,768,288]{1,2,0:T(8,128)(2,1)} %copy.50), calls=%async_computation.1 | async-start | bytes 3538944 | tf_op jit(solution)/shard_map/all_to_all | solution.py:459
  250.9 366.7 %reduce-scatter.10.cloned.1.call-start = ((), (), s32[]{:S(2)}) async-start(), calls=%async_computation.12 | async-start | bytes 1492992
  383.6 41.7 %collective-permute-start.31 = (bf16[2304,1152]{1,0:T(8,128)(2,1)}, bf16[2304,1152]{1,0:T(8,128)(2,1)}, u32[]{:S(2)}, u32[]{:S(2)}) collective-permute-start(bf16[2304,1152]{1,0:T(8,128)(2,1)} %constant_dynamic-slice_fusion), channel_id=1, source_target_pairs={{0,8},{8,0},{1,9},{9,1},{2,10},{10,2},{3,11},{11,3},{4,12},{12,4},... | collective-permute-start | bytes 15925256 | tf_op jit(solution)/shard_map/ppermute | solution.py:257
  407.6 25.8 %collective-permute-start.12 = (bf16[24,1152]{1,0:T(8,128)(2,1)S(1)}, bf16[24,1152]{1,0:T(8,128)(2,1)S(1)}, u32[]{:S(2)}, u32[]{:S(2)}) collective-permute-start(bf16[24,1152]{1,0:T(8,128)(2,1)S(1)} %multiply_convert_fusion), channel_id=1, source_target_pairs={{0,8},{8,0},{1,9},{9,1},{2,10},{10,2},{3,11},{11,3},{4,12},{12,4},... | collective-permute-start | bytes 165896 | tf_op jit(solution)/shard_map/ppermute | solution.py:257
  420.8 42.7 %all-to-all-start.2 = ((bf16[4,768,288]{1,2,0:T(8,128)(2,1)}), bf16[4,768,288]{1,2,0:T(8,128)(2,1)}, u32[]{:S(2)}, u32[]{:S(2)}) async-start(bf16[4,768,288]{1,2,0:T(8,128)(2,1)} %bitcast.161), calls=%async_computation.2 | async-start | bytes 3538944 | tf_op jit(solution)/shard_map/all_to_all | solution.py:498
  425.3 351.7 %reduce-scatter.8.cloned.1.call-start = ((), (), s32[]{:S(2)}) async-start(), calls=%async_computation.11 | async-start | bytes 5971968 | tf_op jit(solution)/shard_map/reduce_scatter | solution.py:360
  433.3 357.7 %reduce-scatter.6.cloned.1.call-start = ((), (), s32[]{:S(2)}) async-start(), calls=%async_computation.10 | async-start | bytes 5971968 | tf_op jit(solution)/shard_map/reduce_scatter | solution.py:360
  433.5 19.8 %collective-permute-start.13 = (bf16[48,1152]{1,0:T(8,128)(2,1)S(1)}, bf16[48,1152]{1,0:T(8,128)(2,1)S(1)}, u32[]{:S(2)}, u32[]{:S(2)}) collective-permute-start(bf16[48,1152]{1,0:T(8,128)(2,1)S(1)} %pad_maximum_fusion.8), channel_id=1, source_target_pairs={{0,16},{16,0},{1,17},{17,1},{2,18},{18,2},{3,19},{19,3},{4,20},{20... | collective-permute-start | bytes 331784 | tf_op jit(solution)/shard_map/ppermute | solution.py:257
  462.0 96.0 %collective-permute-start.28 = (bf16[2304,1152]{1,0:T(8,128)(2,1)}, bf16[2304,1152]{1,0:T(8,128)(2,1)}, u32[]{:S(2)}, u32[]{:S(2)}) collective-permute-start(bf16[2304,1152]{1,0:T(8,128)(2,1)} %constant_dynamic-slice_fusion.2), channel_id=1, source_target_pairs={{0,8},{8,0},{1,9},{9,1},{2,10},{10,2},{3,11},{11,3},{4,12},{12,4},... | collective-permute-start | bytes 15925256 | tf_op jit(solution)/shard_map/ppermute | solution.py:257
  543.8 70.0 %collective-permute-start.16 = (bf16[448,1152]{1,0:T(8,128)(2,1)}, bf16[448,1152]{1,0:T(8,128)(2,1)}, u32[]{:S(2)}, u32[]{:S(2)}) collective-permute-start(bf16[448,1152]{1,0:T(8,128)(2,1)} %select_bitcast_fusion), channel_id=1, source_target_pairs={{0,4},{4,0},{1,5},{5,1},{2,6},{6,2},{3,7},{7,3},{8,12},{12,8},{9,1... | collective-permute-start | bytes 3096584 | tf_op jit(solution)/shard_map/ppermute | solution.py:257
  567.3 60.0 %collective-permute-start.5 = (bf16[2,384,1152]{2,1,0:T(8,128)(2,1)}, bf16[2,384,1152]{2,1,0:T(8,128)(2,1)}, u32[]{:S(2)}, u32[]{:S(2)}) collective-permute-start(bf16[2,384,1152]{2,1,0:T(8,128)(2,1)} %pad_maximum_fusion.2), channel_id=1, source_target_pairs={{0,1},{1,0},{2,3},{3,2},{4,5},{5,4},{6,7},{7,6},{8,9},{9,8},{10,11... | collective-permute-start | bytes 5308424 | tf_op jit(solution)/shard_map/ppermute | solution.py:257
  620.5 75.9 %collective-permute-start.7 = (bf16[2,384,1152]{2,1,0:T(8,128)(2,1)S(1)}, bf16[2,384,1152]{2,1,0:T(8,128)(2,1)S(1)}, u32[]{:S(2)}, u32[]{:S(2)}) collective-permute-start(bf16[2,384,1152]{2,1,0:T(8,128)(2,1)S(1)} %pad_maximum_fusion.3), channel_id=1, source_target_pairs={{0,2},{1,3},{2,0},{3,1},{4,6},{5,7},{6,4},{7,5},{8,10},{9,11},{10,... | collective-permute-start | bytes 5308424 | tf_op jit(solution)/shard_map/ppermute | solution.py:257
  629.0 86.3 %collective-permute-start.6 = (bf16[384,1152]{1,0:T(8,128)(2,1)S(1)}, bf16[384,1152]{1,0:T(8,128)(2,1)S(1)}, u32[]{:S(2)}, u32[]{:S(2)}) collective-permute-start(bf16[384,1152]{1,0:T(8,128)(2,1)S(1)} %fusion.16), channel_id=1, source_target_pairs={{0,2},{1,3},{2,0},{3,1},{4,6},{5,7},{6,4},{7,5},{8,10},{9,11},{10,... | collective-permute-start | bytes 2654216 | tf_op jit(solution)/shard_map/ppermute | solution.py:257
  640.1 79.0 %collective-permute-start.19 = (bf16[224,1152]{1,0:T(8,128)(2,1)S(1)}, bf16[224,1152]{1,0:T(8,128)(2,1)S(1)}, u32[]{:S(2)}, u32[]{:S(2)}) collective-permute-start(bf16[224,1152]{1,0:T(8,128)(2,1)S(1)} %add_convert_fusion.7), channel_id=1, source_target_pairs={{0,8},{8,0},{1,9},{9,1},{2,10},{10,2},{3,11},{11,3},{4,12},{12,4},... | collective-permute-start | bytes 1548296 | tf_op jit(solution)/shard_map/ppermute | solution.py:257
  717.6 28.8 %collective-permute-start.8 = (bf16[384,1152]{1,0:T(8,128)(2,1)S(1)}, bf16[384,1152]{1,0:T(8,128)(2,1)S(1)}, u32[]{:S(2)}, u32[]{:S(2)}) collective-permute-start(bf16[384,1152]{1,0:T(8,128)(2,1)S(1)} %get-tuple-element.48), channel_id=1, source_target_pairs={{0,1},{1,0},{2,3},{3,2},{4,5},{5,4},{6,7},{7,6},{8,9},{9,8},{10,11... | collective-permute-start | bytes 2654216 | tf_op jit(solution)/shard_map/ppermute | solution.py:257
  (73 other events, 773.8 us)
Sparse Core Ops, SparseCore 0:
  10.8 70.9 all-gather.3
  84.6 116.9 all-gather.5
  204.3 108.6 all-gather.7
  407.8 66.5 reduce-scatter.9
  477.8 127.0 reduce-scatter.7
  608.4 143.5 reduce-scatter.5

commit v3 on v2

--- a/solution.py
+++ b/solution.py
@@ -197,56 +197,76 @@
     )(single, qkv, grad_mix)
 
 
-def mlp_kernel(x_ref, g_ref, w1_ref, w2_ref, b1_ref, out_ref, gin_ref, d1_ref, d2_ref, db_ref):
+def mlp_kernel(
+    x_ref, xo_ref, g_ref, go_ref, w1_ref, w2_ref, b1_ref,
+    out_ref, outo_ref, gin_ref, gino_ref, d1_ref, d2_ref, db_ref,
+    x_s, g_s, acc_s, gacc_s,
+):
+    rows = x_ref.shape[0]
+
     @pl.when(pl.program_id(0) == 0)
     def _():
-        out_ref[...] = jnp.zeros_like(out_ref)
-        gin_ref[...] = jnp.zeros_like(gin_ref)
+        x_s[:rows], x_s[rows:] = x_ref[...], xo_ref[...]
+        g_s[:rows], g_s[rows:] = g_ref[...], go_ref[...]
+        for ref in (out_ref, gin_ref, acc_s, gacc_s):
+            ref[...] = jnp.zeros_like(ref)
 
     root = math.sqrt(2.0 / math.pi)
-    x, g, w1, w2 = x_ref[...], g_ref[...], w1_ref[...], w2_ref[...]
-    pre = lax.dot_general(x, w1, NT, preferred_element_type=F32) + b1_ref[0]
-    grad_hidden = lax.dot_general(g, w2, NT, preferred_element_type=F32)
+    w1, w2 = w1_ref[...], w2_ref[...]
+    pre = lax.dot_general(x_s[...], w1, NT, preferred_element_type=F32) + b1_ref[0]
+    grad_hidden = lax.dot_general(g_s[...], w2, NT, preferred_element_type=F32)
     square = pre * pre
     bent = jnp.tanh(root * (pre * (1.0 + 0.044715 * square)))
     half = 0.5 * (1.0 + bent)
     slope = half + (0.5 * root) * pre * (1.0 - bent * bent) * (1.0 + (3 * 0.044715) * square)
     hidden = (pre * half).astype(BF16)
     grad_pre = (grad_hidden * slope).astype(BF16)
-    out_ref[...] += jnp.dot(hidden, w2, preferred_element_type=F32)
-    gin_ref[...] += jnp.dot(grad_pre, w1, preferred_element_type=F32)
-    d2_ref[...] = lax.dot_general(hidden, g, TN, preferred_element_type=F32).astype(BF16)
-    d1_ref[...] = lax.dot_general(grad_pre, x, TN, preferred_element_type=F32).astype(BF16)
+    out_ref[...] += jnp.dot(hidden[:rows], w2, preferred_element_type=F32)
+    acc_s[...] += jnp.dot(hidden[rows:], w2, preferred_element_type=F32)
+    gin_ref[...] += jnp.dot(grad_pre[:rows], w1, preferred_element_type=F32)
+    gacc_s[...] += jnp.dot(grad_pre[rows:], w1, preferred_element_type=F32)
+    d2_ref[...] = lax.dot_general(hidden, g_s[...], TN, preferred_element_type=F32).astype(BF16)
+    d1_ref[...] = lax.dot_general(grad_pre, x_s[...], TN, preferred_element_type=F32).astype(BF16)
     db_ref[0] = jnp.sum(grad_pre.astype(F32), axis=0, keepdims=True)
 
-
-def mlp(x, g, w1, w2, b1):
+    @pl.when(pl.program_id(0) == pl.num_programs(0) - 1)
+    def _():
+        outo_ref[...] = acc_s[...].astype(BF16)
+        gino_ref[...] = gacc_s[...].astype(BF16)
+
+
+def mlp(x, x_other, g, g_other, w1, w2, b1):
     rows, width = x.shape
     units = w1.shape[0]
-    tile = next(t for t in (512, 256, 128) if units % t == 0)
+    tile = next(t for t in (256, 128) if units % t == 0)
     tiles = units // tile
+    given = pl.BlockSpec((rows, width), lambda f: (0, 0), pipeline_mode=pl.Buffered(1))
     whole = pl.BlockSpec((rows, width), lambda f: (0, 0))
     piece = pl.BlockSpec((tile, width), lambda f: (f, 0))
     line = pl.BlockSpec((1, 1, tile), lambda f: (f, 0, 0))
     return pl.pallas_call(
         mlp_kernel,
         grid=(tiles,),
-        in_specs=[whole, whole, piece, piece, line],
-        out_specs=[whole, whole, piece, piece, line],
+        in_specs=[given] * 4 + [piece, piece, line],
+        out_specs=[whole] * 4 + [piece, piece, line],
         out_shape=[
             jax.ShapeDtypeStruct((rows, width), F32),
+            jax.ShapeDtypeStruct((rows, width), BF16),
             jax.ShapeDtypeStruct((rows, width), F32),
+            jax.ShapeDtypeStruct((rows, width), BF16),
             jax.ShapeDtypeStruct((units, width), BF16),
             jax.ShapeDtypeStruct((units, width), BF16),
             jax.ShapeDtypeStruct((tiles, 1, tile), F32),
         ],
+        scratch_shapes=[pltpu.VMEM((2 * rows, width), BF16)] * 2
+        + [pltpu.VMEM((rows, width), F32)] * 2,
         cost_estimate=pl.CostEstimate(
-            flops=12 * rows * width * units,
-            bytes_accessed=8 * units * width + 12 * rows * width,
-            transcendentals=rows * units,
+            flops=24 * rows * width * units,
+            bytes_accessed=8 * units * width + 20 * rows * width,
+            transcendentals=2 * rows * units,
         ),
         name="mlp",
-    )(x, g, w1, w2, b1.reshape(tiles, 1, tile))
+    )(x, x_other, g, g_other, w1, w2, b1.reshape(tiles, 1, tile))
 
 
 def xor_pairs(size, mask):
@@ -353,6 +373,54 @@
     other = swap(own, CORE, 2, 1)
     first = lax.axis_index(CORE) == 0
     return jnp.concatenate([jnp.where(first, own, other), jnp.where(first, other, own)])
+
+
+def gather_weight(shard, planes):
+    if planes != 2:
+        return core_half(lax.all_gather(core_half(shard), SPREAD, axis=0, tiled=True))
+    quarter = shard.shape[0] // 4
+    at = (lax.axis_index(OUTER) * 2 + lax.axis_index(CORE)) * quarter
+    return core_half(
+        lax.all_gather(lax.dynamic_slice_in_dim(shard, at, quarter), SPREAD, axis=0, tiled=True)
+    )
+
+
+def cross_planes(mine, planes):
+    return jnp.concatenate([mine, swap(mine, OUTER, 2, 1)]) if planes == 2 else mine
+
+
+def order_units(rows, planes):
+    heads, units = rows.shape
+    core = lax.axis_index(CORE)
+    if planes != 2:
+        halves = jnp.transpose(rows.reshape(heads, 2, units // 2), (1, 0, 2))
+        return jnp.where(core == 0, halves[0], halves[1]).reshape(-1)
+    quarters = jnp.transpose(rows.reshape(heads, 2, 2, units // 4), (2, 1, 0, 3))
+    quarters = jnp.where(core == 0, quarters[0], quarters[1])
+    return jnp.where(lax.axis_index(OUTER) == 0, quarters, quarters[::-1]).reshape(-1)
+
+
+def restore_units(mine, heads, planes):
+    core = lax.axis_index(CORE)
+    if planes != 2:
+        mine = mine.reshape(heads, 1, -1)
+    else:
+        mine = mine.reshape(2, heads, -1)
+        mine = jnp.where(lax.axis_index(OUTER) == 0, mine, mine[::-1])
+        mine = jnp.transpose(mine, (1, 0, 2))
+    none = jnp.zeros_like(mine)
+    both = jnp.stack([jnp.where(core == 0, mine, none), jnp.where(core == 0, none, mine)], axis=2)
+    return both.reshape(heads, -1)
+
+
+def join_planes(quarter):
+    across = swap(quarter, OUTER, 2, 1)
+    first = lax.axis_index(OUTER) == 0
+    pair = jnp.stack([jnp.where(first, across, quarter), jnp.where(first, quarter, across)])
+    beside = swap(pair, CORE, 2, 1)
+    first = lax.axis_index(CORE) == 0
+    whole = jnp.stack([jnp.where(first, pair, beside), jnp.where(first, beside, pair)], axis=1)
+    return whole.reshape(-1, quarter.shape[1]).astype(F32)
 
 
 def scatter_weight(value):
@@ -399,10 +467,10 @@
     heads = part_size * cols // HEAD_DIM
     head_at = lax.axis_index(HEAD)
 
+    fc1_mine = gather_weight(w_fc1.T, outer_size)
+    fc2_mine = gather_weight(w_fc2, outer_size)
     proj_half = cols // 2
     proj_full = lax.all_gather(core_half(w_proj), SPREAD, axis=0, tiled=True)
-    fc1_full = lax.all_gather(core_half(w_fc1.T), SPREAD, axis=0, tiled=True)
-    fc2_full = lax.all_gather(core_half(w_fc2), SPREAD, axis=0, tiled=True)
     qkv_own = jnp.transpose(w_qkv, (1, 2, 0)).reshape(3 * cols, width)
     if part_size == 2:
         qkv_other = swap(qkv_own, PART, 2, 1)
@@ -429,9 +497,7 @@
         axis=1,
     )
     mod_got = lax.all_to_all(mod_sent, HEAD, split_axis=0, concat_axis=0, tiled=True)
-    bias_fc1 = jnp.transpose(
-        mod_got[:, units, :ff_here].reshape(head_size, 2, ff_here // 2), (1, 0, 2)
-    ).reshape(-1)
+    bias_fc1 = order_units(mod_got[:, units, :ff_here], outer_size)
     bias_parts = mod_got[:, units + 1, : 3 * cols].reshape(part_size, group_size, 3 * cols)
     qkv_bias = lax.dynamic_slice_in_dim(
         bias_parts, lax.axis_index(GROUP), 1, axis=1
@@ -449,6 +515,9 @@
     normed_a, inverse_a = layer_norm(resid)
     attn_in = flat((normed_a * (1.0 + scale_a) + shift_a).astype(BF16))
     gathered = gather_group(attn_in, group_size)
+    gathered, fc1_mine, fc2_mine = lax.optimization_barrier((gathered, fc1_mine, fc2_mine))
+    fc1_here = cross_planes(fc1_mine, outer_size)
+    fc2_here = cross_planes(fc2_mine, outer_size)
     qkv = (lax.dot_general(gathered, qkv_weight, NT, preferred_element_type=F32) + qkv_bias).astype(
         BF16
     )
@@ -469,13 +538,27 @@
     mlp_in = flat((normed_m * (1.0 + scale_m) + shift_m).astype(BF16))
     cotan = by_unit(cotangent.astype(F32))
     grad_branch_m = flat((gate_m * cotan).astype(BF16))
-    branch_m, grad_mlp_in, grad_fc1, grad_fc2, grad_b1 = mlp(
-        mlp_in, grad_branch_m, fc1_full, fc2_full, bias_fc1
-    )
-    grad_fc2 = scatter_weight(grad_fc2)
-    grad_fc1 = scatter_weight(grad_fc1)
-    branch_m = by_unit(branch_m) + b_fc2.astype(F32)
-    grad_mlp_in = by_unit(grad_mlp_in)
+    branch_m, branch_beside, grad_mlp_in, grad_beside, grad_fc1, grad_fc2, grad_b1 = mlp(
+        mlp_in,
+        swap(mlp_in, CORE, 2, 1),
+        grad_branch_m,
+        swap(grad_branch_m, CORE, 2, 1),
+        fc1_here,
+        fc2_here,
+        bias_fc1,
+    )
+    grad_mlp_in = by_unit(grad_mlp_in + swap(grad_beside, CORE, 2, 1).astype(F32))
+    branch_m = by_unit(
+        branch_m + swap(branch_beside, CORE, 2, 1).astype(F32) + b_fc2.astype(F32)
+    )
+    if outer_size == 2:
+        half = grad_fc2.shape[0] // 2
+        crossed_fc2 = swap(grad_fc2[:half], OUTER, 2, 1)
+        sent_fc1, crossed_fc2 = lax.optimization_barrier((grad_fc1[:half], crossed_fc2))
+        crossed_fc1 = swap(sent_fc1, OUTER, 2, 1)
+        grad_fc2 = (grad_fc2[half:].astype(F32) + crossed_fc2.astype(F32)).astype(BF16)
+        grad_fc1 = (grad_fc1[half:].astype(F32) + crossed_fc1.astype(F32)).astype(BF16)
+    grad_b1 = restore_units(grad_b1.reshape(-1), head_size, outer_size)
     output = flat((mid + gate_m * branch_m).astype(BF16))
     grad_mid = cotan + norm_back(grad_mlp_in * (1.0 + scale_m), normed_m, inverse_m)
     grad_branch_a = flat((gate_a * grad_mid).astype(BF16))
@@ -490,16 +573,20 @@
         bias_sums = sum_axis(bias_sums, axis, size)
     grad_b_proj, grad_b_fc2 = bias_sums[0], bias_sums[1]
     grad_b1 = lax.dynamic_slice_in_dim(
-        bias_sums[2:].reshape(2, head_size, ff_here // 2), head_at, 1, axis=1
+        bias_sums[2:].reshape(head_size, ff_here), head_at, 1
     ).reshape(-1)
     grad_mix = lax.dot_general(grad_branch_a, proj_full, NT, preferred_element_type=F32)
     grad_mix = grad_mix.astype(BF16).reshape(rows, 2, part_size, group_size, proj_half)
     grad_mix = jnp.transpose(grad_mix, (3, 0, 2, 1, 4)).reshape(group_size, rows, -1)
     grad_mix = lax.all_to_all(grad_mix, GROUP, split_axis=0, concat_axis=0)
+    grad_mix, grad_fc2 = lax.optimization_barrier((grad_mix, grad_fc2))
     grad_proj = lax.dot_general(mix, grad_branch_a, TN, preferred_element_type=F32).astype(BF16)
     grad_proj = scatter_weight(grad_proj)
+    scattered_fc2 = lax.psum_scatter(grad_fc2, HEAD, scatter_dimension=0, tiled=True)
+    scattered_fc1 = lax.psum_scatter(grad_fc1, HEAD, scatter_dimension=0, tiled=True)
     grad_qkv = attend_back(single, qkv, grad_mix.reshape(-1, heads * HEAD_DIM), heads, cols)
     attn_grad_part = jnp.dot(grad_qkv, qkv_weight, preferred_element_type=F32).astype(BF16)
+    attn_grad_part, grad_qkv = lax.optimization_barrier((attn_grad_part, grad_qkv))
     grad_attn_in = by_unit(scatter_group(attn_grad_part, group_size))
 
     grad_w_qkv = lax.dot_general(grad_qkv, gathered, TN, preferred_element_type=F32)
@@ -525,8 +612,12 @@
     grad_bias_qv = jnp.stack([grad_bias[:cols], grad_bias[2 * cols :]])
     grad_w_qkv = jnp.transpose(grad_w_qkv[: 3 * cols].reshape(3, cols, width), (2, 0, 1))
 
-    grad_fc2 = join_cores(sum_outer(grad_fc2, outer_size)).astype(F32)
-    grad_fc1 = join_cores(sum_outer(grad_fc1, outer_size)).astype(F32).T
+    if outer_size == 2:
+        grad_fc2 = join_planes(scattered_fc2)
+        grad_fc1 = join_planes(scattered_fc1).T
+    else:
+        grad_fc2 = join_cores(sum_outer(scattered_fc2, outer_size)).astype(F32)
+        grad_fc1 = join_cores(sum_outer(scattered_fc1, outer_size)).astype(F32).T
     grad_proj = join_cores(sum_outer(grad_proj, outer_size)).astype(F32)
 
     grad_tokens = flat(

time: 835 us -> 894 us (1.071)
  waiting for transfers between devices: 386 us -> 406 us
  other arithmetic: 86.9 us -> 98.7 us
  Pallas kernels: 165 us -> 174 us
    ppermute x34 -> x40, waiting for transfers between devices: 328 us -> 374 us  [swap(): return lax.ppermute(value, axis, xor_pairs(size, mask))]
    all_to_all x1, waiting for transfers between devices: 37.6 us -> 13.1 us  [local(): lax.all_to_all(mix_part.reshape(group_size, rows, heads * HEAD_DIM), GROU...]
    convert_element_type x3 -> x1, other arithmetic: 17.4 us -> 3.09 us  [scatter_weight(): value = sum_cores(value).astype(BF16)]
    dynamic_slice x3 -> x1, local copies, waits for them, and re-layouts: 10.6 us -> 0.1 us  [sum_cores(): lax.dynamic_slice_in_dim(value, (1 - lax.axis_index(CORE)) * half, half)]
    unnamed x116 -> x105, local copies, waits for them, and re-layouts: 18.4 us -> 8.48 us
    pallas_call x1, Pallas kernels: 65.3 us -> 74.5 us  [mlp(): pl.pallas_call(mlp_kernel, grid=(tiles,), in_specs=[given] * 4 + [piece,...]
    concatenate x0 -> x2, other arithmetic: none -> 9.07 us  [cross_planes(): jnp.concatenate([mine, swap(mine, OUTER, 2, 1)])]
    ppermute x34 -> x40, starting transfers between devices: 24.5 us -> 29.4 us  [swap(): return lax.ppermute(value, axis, xor_pairs(size, mask))]
  transfers between devices with their start and end apart: 44 -> 50, of which waited for: 22 -> 24; matrix products, arithmetic and copies ran while one was open for 22% -> 25% of each run, Pallas kernels for 12% -> 11%
where the time goes in v3:
time: 894 us; the launch traced here: 878 us
  waiting for transfers between devices  406 us (45%)
  Pallas kernels  174 us (19%)
  other arithmetic  98.7 us (11%)
  local copies, waits for them, and re-layouts  75.8 us (8%)
  matrix products  57.8 us (6%)
  starting transfers between devices  49.3 us (6%)
  between operations  15.8 us (2%)
    ppermute x40, waiting for transfers between devices, swap(): return lax.ppermute(value, axis, xor_pairs(size, mask))  374 us
    pallas_call x1, Pallas kernels, mlp(): pl.pallas_call(mlp_kernel, grid=(tiles,), in_specs=[given] * 4 + [piece,...  74.5 us
    pallas_call x1, Pallas kernels, attend_back(): pl.pallas_call(functools.partial(attend_back_kernel, heads, cols), grid_s...  59.4 us
    pallas_call x1, Pallas kernels, attend(): pl.pallas_call(functools.partial(attend_kernel, heads, cols), grid_spec=p...  40.2 us
    ppermute x40, starting transfers between devices, swap(): return lax.ppermute(value, axis, xor_pairs(size, mask))  29.4 us
  transfers between devices with their start and end apart: 50, of which 24 were waited for; matrix products, arithmetic and copies ran while one was open for 25% of the time, Pallas kernels for 11%

profile of v3, /device:TPU:0, one launch (start us, length us, event | category | flops | bytes accessed | tf_op | source)
XLA Modules:
  0.0 878.0 jit_solution(14166840095244019542)
XLA Ops:
  15.4 7.3 all-to-all-start
  26.6 11.4 %all-to-all-done = f32[8,5,864]{2,1,0:T(8,128)S(1)} async-done(((f32[8,5,864]{2,1,0:T(8,128)}), f32[8,5,864]{2,1,0:T(8,128)S(1)}, u32[]{:S(2)}, u32[]{:S(2)}) %all-to-all-start) | async-done | bytes 138272 | tf_op jit(solution)/shard_map/all_to_all | solution.py:499
  50.7 85.2 %collective-permute-done.1 = bf16[768,1152]{1,0:T(8,128)(2,1)} collective-permute-done((bf16[768,1152]{1,0:T(8,128)(2,1)}, bf16[768,1152]{1,0:T(8,128)(2,1)}, u32[]{:S(2)}, u32[]{:S(2)}) %collective-permute-start.1) | collective-permute-done | bytes 1769504 | tf_op jit(solution)/shard_map/ppermute | solution.py:277
  148.0 19.8 %collective-permute-done.2 = bf16[384,1152]{1,0:T(8,128)(2,1)S(1)} collective-permute-done((bf16[384,1152]{1,0:T(8,128)(2,1)S(1)}, bf16[384,1152]{1,0:T(8,128)(2,1)S(1)}, u32[]{:S(2)}, u32[]{:S(2)}) %collective-permute-start.2) | collective-permute-done | bytes 884768 | tf_op jit(solution)/shard_map/ppermute | solution.py:277
  168.8 8.9 %collective-permute-done.3 = bf16[384,1152]{1,0:T(8,128)(2,1)S(1)} collective-permute-done((bf16[384,1152]{1,0:T(8,128)(2,1)S(1)}, bf16[384,1152]{1,0:T(8,128)(2,1)S(1)}, u32[]{:S(2)}, u32[]{:S(2)}) %collective-permute-start.3) | collective-permute-done | bytes 884768 | tf_op jit(solution)/shard_map/ppermute | solution.py:277
  185.8 11.9 %add_convert_fusion.qkv_ref = bf16[3072,864]{1,0:T(8,128)(2,1)} fusion(f32[864]{0:T(1024)S(1)} %add.380, bf16[3072,1152]{1,0:T(8,128)(2,1)} %constant_dynamic-update-slice_fusion.6, bf16[432,1152]{1,0:T(8,128)(2,1)S(1)} %copy-done.28, bf16[432,1152]{1,0:T(8,128)(2,1)S(1)} %copy-done.26), kind=kOutput, calls=%fused_computation.3 | convolution fusion | flops 6124584960 | bytes 14380416 | tf_op jit(solution)/shard_map/dot_general | solution.py:521
  197.7 40.2 %attend.1 = bf16[3072,288]{1,0:T(8,128)(2,1)} custom-call(s32[3]{0:T(128)} %compare_convert_fusion.single_ref, bf16[3072,864]{1,0:T(8,128)(2,1)} %add_convert_fusion.qkv_ref), custom_call_target="tpu_custom_call" | custom-call | flops 6442450944 | bytes 7077888 | tf_op jit(solution)/shard_map/attend/pallas_call | solution.py:91
  253.4 13.1 %all-to-all-done.1 = bf16[4,768,288]{1,2,0:T(8,128)(2,1)} async-done(((bf16[4,768,288]{1,2,0:T(8,128)(2,1)}), bf16[4,768,288]{1,2,0:T(8,128)(2,1)}, u32[]{:S(2)}, u32[]{:S(2)}) %all-to-all-start.1) | async-done | bytes 1769504 | tf_op jit(solution)/shard_map/all_to_all | solution.py:528
  269.3 7.8 fusion.49
  278.9 28.6 %collective-permute-done.8 = bf16[1152,1152]{1,0:T(8,128)(2,1)} collective-permute-done((bf16[1152,1152]{1,0:T(8,128)(2,1)}, bf16[1152,1152]{1,0:T(8,128)(2,1)}, u32[]{:S(2)}, u32[]{:S(2)}) %collective-permute-start.8) | collective-permute-done | bytes 2654240 | tf_op jit(solution)/shard_map/ppermute | solution.py:277
  312.0 52.3 %collective-permute-done.7 = bf16[1152,1152]{1,0:T(8,128)(2,1)} collective-permute-done((bf16[1152,1152]{1,0:T(8,128)(2,1)}, bf16[1152,1152]{1,0:T(8,128)(2,1)}, u32[]{:S(2)}, u32[]{:S(2)}) %collective-permute-start.7) | collective-permute-done | bytes 2654240 | tf_op jit(solution)/shard_map/ppermute | solution.py:277
  368.9 74.5 %mlp.1 = (f32[768,1152]{1,0:T(8,128)}, bf16[768,1152]{1,0:T(8,128)(2,1)}, f32[768,1152]{1,0:T(8,128)}, bf16[768,1152]{1,0:T(8,128)(2,1)}, bf16[2304,1152]{1,0:T(...) custom-call(bf16[768,1152]{1,0:T(8,128)(2,1)} %copy-done.23, ...), custom_call_target="tpu_custom_call" | custom-call | flops 48922361856 | bytes 38928384 | tf_op jit(solution)/shard_map/mlp/pallas_call | solution.py:247
  462.8 17.0 %convert_reduce_fusion.1 = (f32[1152]{0:T(1024)S(1)}, bf16[768,1152]{1,0:T(8,128)(2,1)}, f32[768,1152]{1,0:T(8,128)}, bf16[768,1152]{1,0:T(8,128)(2,1)}, f32[768,1152]{1,0:T(8,128)}) fusion(f32[3,1152]{1,0:T(4,128)S(1)} %bitcast.207, f32[768]{0:T(1024)S(1)} %broadcast_multiply_fusion.2, f32[768,1152]{1,0:T(8,128)S(1)} %copy-done.2, ...), kind=kLoop, calls=%fused_computation.33 | loop fusion | flops 16808832 | bytes 24835584 | tf_op jit(solution)/shard_map/reduce_sum | solution.py:567
  488.2 27.1 %collective-permute-done.31 = f32[6,1152]{1,0:T(8,128)S(1)} collective-permute-done((f32[6,1152]{1,0:T(8,128)S(1)}, f32[6,1152]{1,0:T(8,128)S(1)}, u32[]{:S(2)}, u32[]{:S(2)}) %collective-permute-start.31) | collective-permute-done | bytes 27680 | tf_op jit(solution)/shard_map/ppermute | solution.py:277
  539.0 14.8 %collective-permute-done.33 = f32[6,1152]{1,0:T(8,128)S(1)} collective-permute-done((f32[6,1152]{1,0:T(8,128)S(1)}, f32[6,1152]{1,0:T(8,128)S(1)}, u32[]{:S(2)}, u32[]{:S(2)}) %collective-permute-start.33) | collective-permute-done | bytes 27680 | tf_op jit(solution)/shard_map/ppermute | solution.py:277
  572.0 59.4 %attend_back.1 = bf16[3072,864]{1,0:T(8,128)(2,1)} custom-call(s32[3]{0:T(128)} %compare_convert_fusion.single_ref, bf16[3072,864]{1,0:T(8,128)(2,1)} %add_convert_fusion.qkv_ref, bf16[3072,288]{1,0:T(8,128)(2,1)} %bitcast.196), custom_call_target="tpu_custom_call" | custom-call | flops 16106127360 | bytes 12386304 | tf_op jit(solution)/shard_map/attend_back/pallas_call | solution.py:178
  631.4 12.1 %convolution_convert_fusion = bf16[3072,1152]{1,0:T(8,128)(2,1)} fusion(bf16[3072,864]{1,0:T(8,128)(2,1)} %attend_back.1, bf16[432,1152]{1,0:T(8,128)(2,1)} %get-tuple-element.83, bf16[432,1152]{1,0:T(8,128)(2,1)S(1)} %copy-done.27), kind=kOutput, calls=%fused_computation.2 | convolution fusion | flops 6122815488 | bytes 14376960 | tf_op jit(solution)/shard_map/dot_general | solution.py:588
  643.6 11.9 %convolution_convert_fusion.2 = bf16[864,1152]{1,0:T(8,128)(2,1)} fusion(bf16[3072,864]{1,0:T(8,128)(2,1)} %attend_back.1, bf16[3072,1152]{1,0:T(8,128)(2,1)} %constant_dynamic-update-slice_fusion.6), kind=kOutput, calls=%fused_computation.48 | convolution fusion | flops 6116290560 | bytes 14376960 | tf_op jit(solution)/shard_map/dot_general | solution.py:592
  672.7 55.6 %collective-permute-done.23 = bf16[448,1152]{1,0:T(8,128)(2,1)} collective-permute-done((bf16[448,1152]{1,0:T(8,128)(2,1)S(1)}, bf16[448,1152]{1,0:T(8,128)(2,1)}, u32[]{:S(2)}, u32[]{:S(2)}) %collective-permute-start.23) | collective-permute-done | bytes 1032224 | tf_op jit(solution)/shard_map/ppermute | solution.py:277
  745.3 10.0 %collective-permute-done.25 = bf16[224,1152]{1,0:T(8,128)(2,1)S(1)} collective-permute-done((bf16[224,1152]{1,0:T(8,128)(2,1)S(1)}, bf16[224,1152]{1,0:T(8,128)(2,1)S(1)}, u32[]{:S(2)}, u32[]{:S(2)}) %collective-permute-start.25) | collective-permute-done | bytes 516128 | tf_op jit(solution)/shard_map/ppermute | solution.py:277
  755.5 21.3 %collective-permute-done.13 = bf16[384,1152]{1,0:T(8,128)(2,1)S(1)} collective-permute-done((bf16[384,1152]{1,0:T(8,128)(2,1)S(1)}, bf16[384,1152]{1,0:T(8,128)(2,1)S(1)}, u32[]{:S(2)}, u32[]{:S(2)}) %collective-permute-start.13) | collective-permute-done | bytes 884768 | tf_op jit(solution)/shard_map/ppermute | solution.py:277
  783.2 22.5 %collective-permute-done.15 = bf16[384,1152]{1,0:T(8,128)(2,1)S(1)} collective-permute-done((bf16[384,1152]{1,0:T(8,128)(2,1)S(1)}, bf16[384,1152]{1,0:T(8,128)(2,1)S(1)}, u32[]{:S(2)}, u32[]{:S(2)}) %collective-permute-start.15) | collective-permute-done | bytes 884768 | tf_op jit(solution)/shard_map/ppermute | solution.py:277
  821.1 7.3 all-to-all-done.3
  849.0 6.3 collective-permute-done.18
  (355 shorter events, 235.9 us)
Async XLA Ops:
  7.2 171.5 %all-gather.6.cloned.1.call-start = ((), (), s32[]{:S(2)}) async-start(), calls=%async_computation.8 | async-start | bytes 5640192 | tf_op jit(solution)/shard_map/all_gather | solution.py:384
  9.2 173.0 %all-gather.4.cloned.1.call-start = ((), (), s32[]{:S(2)}) async-start(), calls=%async_computation.7 | async-start | bytes 5640192 | tf_op jit(solution)/shard_map/all_gather | solution.py:384
  22.7 246.6 %all-gather.8.cloned.1.call-start = ((), (), s32[]{:S(2)}) async-start(), calls=%async_computation.9 | async-start | bytes 2820096 | tf_op jit(solution)/shard_map/all_gather | solution.py:473
  44.5 91.4 %collective-permute-start.1 = (bf16[768,1152]{1,0:T(8,128)(2,1)}, bf16[768,1152]{1,0:T(8,128)(2,1)}, u32[]{:S(2)}, u32[]{:S(2)}) collective-permute-start(bf16[768,1152]{1,0:T(8,128)(2,1)} %get-tuple-element.115), channel_id=1, source_target_pairs={{0,2},{1,3},{2,0},{3,1},{4,6},{5,7},{6,4},{7,5},{8,10},{9,11},{10,... | collective-permute-start | bytes 5308424 | tf_op jit(solution)/shard_map/ppermute | solution.py:277
  44.5 93.7 %collective-permute-start = (bf16[768,1152]{1,0:T(8,128)(2,1)}, bf16[768,1152]{1,0:T(8,128)(2,1)}, u32[]{:S(2)}, u32[]{:S(2)}) collective-permute-start(bf16[768,1152]{1,0:T(8,128)(2,1)} %get-tuple-element.115), channel_id=1, source_target_pairs={{0,1},{1,0},{2,3},{3,2},{4,5},{5,4},{6,7},{7,6},{8,9},{9,8},{10,11... | collective-permute-start | bytes 5308424 | tf_op jit(solution)/shard_map/ppermute | solution.py:277
  45.5 94.1 %collective-permute-start.4 = (bf16[432,1152]{1,0:T(8,128)(2,1)S(1)}, bf16[432,1152]{1,0:T(8,128)(2,1)}, u32[]{:S(2)}, u32[]{:S(2)}) collective-permute-start(bf16[432,1152]{1,0:T(8,128)(2,1)S(1)} %bitcast.200), channel_id=1, source_target_pairs={{0,4},{4,0},{1,5},{5,1},{2,6},{6,2},{3,7},{7,3},{8,12},{12,8},{9,1... | collective-permute-start | bytes 2985992 | tf_op jit(solution)/shard_map/ppermute | solution.py:277
  137.2 30.7 %collective-permute-start.2 = (bf16[384,1152]{1,0:T(8,128)(2,1)S(1)}, bf16[384,1152]{1,0:T(8,128)(2,1)S(1)}, u32[]{:S(2)}, u32[]{:S(2)}) collective-permute-start(bf16[384,1152]{1,0:T(8,128)(2,1)S(1)} %slice.141), channel_id=1, source_target_pairs={{0,1},{1,0},{2,3},{3,2},{4,5},{5,4},{6,7},{7,6},{8,9},{9,8},{10,11... | collective-permute-start | bytes 2654216 | tf_op jit(solution)/shard_map/ppermute | solution.py:277
  139.5 38.3 %collective-permute-start.3 = (bf16[384,1152]{1,0:T(8,128)(2,1)S(1)}, bf16[384,1152]{1,0:T(8,128)(2,1)S(1)}, u32[]{:S(2)}, u32[]{:S(2)}) collective-permute-start(bf16[384,1152]{1,0:T(8,128)(2,1)S(1)} %slice.142), channel_id=1, source_target_pairs={{0,2},{1,3},{2,0},{3,1},{4,6},{5,7},{6,4},{7,5},{8,10},{9,11},{10,... | collective-permute-start | bytes 2654216 | tf_op jit(solution)/shard_map/ppermute | solution.py:277
  246.7 60.8 %collective-permute-start.8 = (bf16[1152,1152]{1,0:T(8,128)(2,1)}, bf16[1152,1152]{1,0:T(8,128)(2,1)}, u32[]{:S(2)}, u32[]{:S(2)}) collective-permute-start(bf16[1152,1152]{1,0:T(8,128)(2,1)} %constant_dynamic-slice_fusion.4), channel_id=1, source_target_pairs={{0,16},{16,0},{1,17},{17,1},{2,18},{18,2},{3,19},{19,3},{4,20},{20... | collective-permute-start | bytes 7962632 | tf_op jit(solution)/shard_map/ppermute | solution.py:277
  248.2 116.1 %collective-permute-start.7 = (bf16[1152,1152]{1,0:T(8,128)(2,1)}, bf16[1152,1152]{1,0:T(8,128)(2,1)}, u32[]{:S(2)}, u32[]{:S(2)}) collective-permute-start(bf16[1152,1152]{1,0:T(8,128)(2,1)} %constant_dynamic-slice_fusion.6), channel_id=1, source_target_pairs={{0,16},{16,0},{1,17},{17,1},{2,18},{18,2},{3,19},{19,3},{4,20},{20... | collective-permute-start | bytes 7962632 | tf_op jit(solution)/shard_map/ppermute | solution.py:277
  253.0 115.9 %collective-permute-start.6 = (bf16[768,1152]{1,0:T(8,128)(2,1)}, bf16[768,1152]{1,0:T(8,128)(2,1)}, u32[]{:S(2)}, u32[]{:S(2)}) collective-permute-start(bf16[768,1152]{1,0:T(8,128)(2,1)} %get-tuple-element.62.g_ref), channel_id=1, source_target_pairs={{0,8},{8,0},{1,9},{9,1},{2,10},{10,2},{3,11},{11,3},{4,12},{12,4},... | collective-permute-start | bytes 5308424 | tf_op jit(solution)/shard_map/ppermute | solution.py:277
  278.9 90.0 %collective-permute-start.5 = (bf16[768,1152]{1,0:T(8,128)(2,1)S(1)}, bf16[768,1152]{1,0:T(8,128)(2,1)}, u32[]{:S(2)}, u32[]{:S(2)}) collective-permute-start(bf16[768,1152]{1,0:T(8,128)(2,1)S(1)} %fusion.10.x_ref), channel_id=1, source_target_pairs={{0,8},{8,0},{1,9},{9,1},{2,10},{10,2},{3,11},{11,3},{4,12},{12,4},... | collective-permute-start | bytes 5308424 | tf_op jit(solution)/shard_map/ppermute | solution.py:277
  450.1 32.6 %collective-permute-start.20 = (bf16[48,1152]{1,0:T(8,128)(2,1)S(1)}, bf16[48,1152]{1,0:T(8,128)(2,1)S(1)}, u32[]{:S(2)}, u32[]{:S(2)}) collective-permute-start(bf16[48,1152]{1,0:T(8,128)(2,1)S(1)} %pad_maximum_fusion.12), channel_id=1, source_target_pairs={{0,16},{16,0},{1,17},{17,1},{2,18},{18,2},{3,19},{19,3},{4,20},{20... | collective-permute-start | bytes 331784 | tf_op jit(solution)/shard_map/ppermute | solution.py:277
  455.0 104.7 %collective-permute-start.11 = (bf16[1152,1152]{1,0:T(8,128)(2,1)}, bf16[1152,1152]{1,0:T(8,128)(2,1)}, u32[]{:S(2)}, u32[]{:S(2)}) collective-permute-start(bf16[1152,1152]{1,0:T(8,128)(2,1)} %slice.119), channel_id=1, source_target_pairs={{0,16},{16,0},{1,17},{17,1},{2,18},{18,2},{3,19},{19,3},{4,20},{20... | collective-permute-start | bytes 7962632 | tf_op jit(solution)/shard_map/ppermute | solution.py:277
  481.3 34.1 %collective-permute-start.31 = (f32[6,1152]{1,0:T(8,128)S(1)}, f32[6,1152]{1,0:T(8,128)S(1)}, u32[]{:S(2)}, u32[]{:S(2)}) collective-permute-start(f32[6,1152]{1,0:T(8,128)S(1)} %add.428), channel_id=1, source_target_pairs={{0,16},{16,0},{1,17},{17,1},{2,18},{18,2},{3,19},{19,3},{4,20},{20... | collective-permute-start | bytes 82952 | tf_op jit(solution)/shard_map/ppermute | solution.py:277
  528.0 40.0 %all-to-all-start.2 = ((bf16[4,768,288]{1,2,0:T(8,128)(2,1)}), bf16[4,768,288]{1,2,0:T(8,128)(2,1)}, u32[]{:S(2)}, u32[]{:S(2)}) async-start(bf16[4,768,288]{1,2,0:T(8,128)(2,1)} %bitcast.190), calls=%async_computation.2 | async-start | bytes 3538944 | tf_op jit(solution)/shard_map/all_to_all | solution.py:581
  532.4 199.7 %reduce-scatter.10.cloned.1.call-start = ((), (), s32[]{:S(2)}) async-start(), calls=%async_computation.12 | async-start | bytes 1492992
  559.7 173.9 %collective-permute-start.35 = (bf16[1152,1152]{1,0:T(8,128)(2,1)}, bf16[1152,1152]{1,0:T(8,128)(2,1)}, u32[]{:S(2)}, u32[]{:S(2)}) collective-permute-start(bf16[1152,1152]{1,0:T(8,128)(2,1)} %slice.118), channel_id=1, source_target_pairs={{0,16},{16,0},{1,17},{17,1},{2,18},{18,2},{3,19},{19,3},{4,20},{20... | collective-permute-start | bytes 7962632 | tf_op jit(solution)/shard_map/ppermute | solution.py:277
  567.9 281.0 %reduce-scatter.8.cloned.1.call-start = ((), (), s32[]{:S(2)}) async-start(), calls=%async_computation.11 | async-start | bytes 2985984 | tf_op jit(solution)/shard_map/reduce_scatter | solution.py:585
  643.6 212.8 %reduce-scatter.6.cloned.1.call-start = ((), (), s32[]{:S(2)}) async-start(), calls=%async_computation.10 | async-start | bytes 2985984 | tf_op jit(solution)/shard_map/reduce_scatter | solution.py:586
  662.6 65.7 %collective-permute-start.23 = (bf16[448,1152]{1,0:T(8,128)(2,1)S(1)}, bf16[448,1152]{1,0:T(8,128)(2,1)}, u32[]{:S(2)}, u32[]{:S(2)}) collective-permute-start(bf16[448,1152]{1,0:T(8,128)(2,1)S(1)} %select_bitcast_fusion), channel_id=1, source_target_pairs={{0,4},{4,0},{1,5},{5,1},{2,6},{6,2},{3,7},{7,3},{8,12},{12,8},{9,1... | collective-permute-start | bytes 3096584 | tf_op jit(solution)/shard_map/ppermute | solution.py:277
  669.3 86.2 %collective-permute-start.14 = (bf16[2,384,1152]{2,1,0:T(8,128)(2,1)}, bf16[2,384,1152]{2,1,0:T(8,128)(2,1)}, u32[]{:S(2)}, u32[]{:S(2)}) collective-permute-start(bf16[2,384,1152]{2,1,0:T(8,128)(2,1)} %pad_maximum_fusion.5), channel_id=1, source_target_pairs={{0,2},{1,3},{2,0},{3,1},{4,6},{5,7},{6,4},{7,5},{8,10},{9,11},{10,... | collective-permute-start | bytes 5308424 | tf_op jit(solution)/shard_map/ppermute | solution.py:277
  671.0 71.6 %collective-permute-start.12 = (bf16[2,384,1152]{2,1,0:T(8,128)(2,1)}, bf16[2,384,1152]{2,1,0:T(8,128)(2,1)}, u32[]{:S(2)}, u32[]{:S(2)}) collective-permute-start(bf16[2,384,1152]{2,1,0:T(8,128)(2,1)} %pad_maximum_fusion.4), channel_id=1, source_target_pairs={{0,1},{1,0},{2,3},{3,2},{4,5},{5,4},{6,7},{7,6},{8,9},{9,8},{10,11... | collective-permute-start | bytes 5308424 | tf_op jit(solution)/shard_map/ppermute | solution.py:277
  744.3 32.5 %collective-permute-start.13 = (bf16[384,1152]{1,0:T(8,128)(2,1)S(1)}, bf16[384,1152]{1,0:T(8,128)(2,1)S(1)}, u32[]{:S(2)}, u32[]{:S(2)}) collective-permute-start(bf16[384,1152]{1,0:T(8,128)(2,1)S(1)} %fusion.16), channel_id=1, source_target_pairs={{0,2},{1,3},{2,0},{3,1},{4,6},{5,7},{6,4},{7,5},{8,10},{9,11},{10,... | collective-permute-start | bytes 2654216 | tf_op jit(solution)/shard_map/ppermute | solution.py:277
  (73 other events, 1093.5 us)
Sparse Core Ops, SparseCore 0:
  10.8 94.7 all-gather.5
  108.4 70.3 all-gather.3
  181.0 43.5 all-gather.7
  568.0 62.5 reduce-scatter.9
  643.7 129.7 reduce-scatter.7
  777.6 78.7 reduce-scatter.5
